TPU v7x, 32 devices: a whole 2x2x4 slice. The times are simulated.
32 devices in a mesh: section: 4 (over z), rep: 8 (over y, x, core).
Axes of the slice: x: 2, y: 2, z: 4, core: 2. Of those that a mesh axis runs over, the one named last changes fastest.
Arguments:
- tokens: bfloat16 [4, 1024, 1024], P(None, 'rep'), may hold values from -6 to 6
- replica_of_row: int32 [4, 1024, 1], P(None, 'rep'), may hold values from 0 to 15; in each aligned block of 128 rows (0 to 127, 128 to 255, ..., all dimensions but the last counted through in order) at most 12 rows name the same one
- widths: int32 [16], replicated, may hold values from 512 to 1024, as said below
- placement: int32 [16], replicated, may hold values from 0 to 23, as said below
- gains: float32 [4, 24, 1024], P('section', 'rep'), may hold values from 0.5 to 1.5
- weights: bfloat16 [4, 24, 1024, 1024], P('section', 'rep'), may hold values from -0.1875 to 0.1875
Outputs:
- final: bfloat16 [4, 1024, 1024], P(None, 'rep', 'section')
Inputs may be any that keep to these rules, and one draw needn't show every extreme that they name: `widths`: multiples of 128 from 512 to 1024. `placement`: distinct slots; slot g lies on index g // 3 of rep. `replica_of_row`: within the 128 tokens of one index of rep in one micro-batch, no replica is named by more than 12 tokens.
All inputs are finite; a program needn't handle non-finite values.
Results may differ from a plain program's by a relative error of at most 0.008.
Values may be sent and summed in bfloat16 or wider, within the bound.
No kernel may reach another device: no remote copies, remote signals or barrier semaphores. Data moves between devices by JAX's collectives and lax.ppermute only.
A program may use at most 64 MiB of HBM per device.

v0:
```python
import jax
import jax.numpy as jnp
from jax import lax
from jax.sharding import PartitionSpec as P

epsilon = 1e-05


def shifted(x, axis, by):
    length = lax.axis_size(axis)
    pairs = [(i, i + by) for i in range(length) if 0 <= i + by < length]
    return lax.ppermute(x, axis, pairs)


def on_device(tokens, replica_of_row, widths, placement, gains, weights):
    batches, row_count, width_max = tokens.shape
    rep_count = lax.axis_size("rep")
    section_count = lax.axis_size("section")
    slot_count = weights.shape[1]
    replica_count = widths.shape[0]
    total_slots = slot_count * rep_count
    capacity = (3 * row_count + 2 * replica_count - 1) // (2 * replica_count)
    section_id = lax.axis_index("section")
    rep_id = lax.axis_index("rep")
    final_section = section_count - 1
    features = jnp.arange(width_max, dtype=jnp.int32)
    replica_ids = jnp.arange(replica_count, dtype=jnp.int32)
    global_ids = rep_id * slot_count + jnp.arange(slot_count, dtype=jnp.int32)
    slot_width = jnp.sum(
        (placement[None, :] == global_ids[:, None]).astype(jnp.int32) * widths[None, :], axis=1
    )
    slot_live = (features[None, :] < slot_width[:, None]).astype(jnp.float32)
    slot_scale = 1.0 / jnp.maximum(slot_width, 1).astype(jnp.float32)
    section_gain = gains[0]
    section_weight = weights[0]
    slot_targets = jnp.arange(total_slots * capacity, dtype=jnp.int32)
    slot_numbers = jnp.arange(total_slots, dtype=jnp.int32)

    def routing(row_replica):
        picked = (row_replica[:, None] == replica_ids[None, :]).astype(jnp.int32)
        slot_of_row = jnp.sum(picked * placement[None, :], axis=1)
        row_width = jnp.sum(picked * widths[None, :], axis=1)
        slot_hits = (slot_of_row[:, None] == slot_numbers[None, :]).astype(jnp.int32)
        earlier = jnp.cumsum(slot_hits, axis=0) - slot_hits
        position = jnp.sum(earlier * slot_hits, axis=1)
        target = slot_of_row * capacity + position
        routing_table = (slot_targets[:, None] == target[None, :]).astype(jnp.bfloat16)
        return (routing_table, row_width)

    def update(buffer):
        float_rows = buffer.astype(jnp.float32)
        mean_square = jnp.sum(float_rows * float_rows, axis=-1) * slot_scale[None, :, None]
        lowered = (
            float_rows
            * lax.rsqrt(mean_square + epsilon)[..., None]
            * section_gain[None, :, None, :]
        ).astype(jnp.bfloat16)
        projected = jnp.einsum(
            "nscd,sde->nsce", lowered, section_weight, preferred_element_type=jnp.float32
        )
        return (float_rows + jax.nn.silu(projected) * slot_live[None, :, None, :]).astype(
            jnp.bfloat16
        )

    def unchanged(buffer):
        return buffer

    tick_count = batches + section_count - 1
    routing_tables, row_widths = jax.vmap(routing)(replica_of_row[:, :, 0])
    entering = jnp.where(
        features[None, None, :] < row_widths[:, :, None], tokens, jnp.zeros((), jnp.bfloat16)
    )
    outgoing = jnp.einsum(
        "mgr,mrd->mgd", routing_tables, entering, preferred_element_type=jnp.float32
    ).astype(jnp.bfloat16)
    outgoing = outgoing.reshape(batches, rep_count, slot_count * capacity, width_max)
    arrived_all = lax.all_to_all(outgoing, "rep", split_axis=1, concat_axis=1, tiled=True)
    arrived_all = arrived_all.reshape(batches, rep_count, slot_count, capacity, width_max)

    def tick(counter, carry):
        incoming, outbuf = carry
        index = counter - section_id
        valid = (index >= 0) & (index < batches)
        clipped = jnp.clip(index, 0, batches - 1)
        first_input = lax.dynamic_index_in_dim(arrived_all, clipped, 0, keepdims=False)
        current = jnp.where(section_id == 0, first_input, incoming)
        updated = lax.cond(valid, update, unchanged, current)
        storing = valid & (section_id == final_section)
        stored = lax.dynamic_update_index_in_dim(outbuf, updated, clipped, 0)
        outbuf = jnp.where(storing, stored, outbuf)
        incoming = shifted(updated, "section", 1)
        return (incoming, outbuf)

    start_slots = jnp.zeros((rep_count, slot_count, capacity, width_max), jnp.bfloat16)
    start_out = jnp.zeros((batches, rep_count, slot_count, capacity, width_max), jnp.bfloat16)
    last_slots, slot_results = lax.fori_loop(0, tick_count, tick, (start_slots, start_out))
    returned = lax.all_to_all(
        slot_results.reshape(batches, rep_count, slot_count * capacity, width_max),
        "rep",
        split_axis=1,
        concat_axis=1,
        tiled=True,
    )
    flat_back = returned.reshape(batches, total_slots * capacity, width_max)
    final_rows = jnp.einsum(
        "mgr,mgd->mrd", routing_tables, flat_back, preferred_element_type=jnp.float32
    ).astype(jnp.bfloat16)
    contribution = jnp.where(
        section_id == final_section, final_rows.astype(jnp.float32), jnp.zeros((), jnp.float32)
    )
    gathered = lax.psum_scatter(
        contribution.astype(jnp.bfloat16), "section", scatter_dimension=2, tiled=True
    )
    return gathered


def solution(mesh):
    placed = (
        P(None, "rep", None),
        P(None, "rep", None),
        P(),
        P(),
        P("section", "rep", None),
        P("section", "rep", None, None),
    )
    return jax.shard_map(
        on_device, mesh=mesh, in_specs=placed, out_specs=P(None, "rep", "section"), check_vma=False
    )
```

profile of v0, /device:TPU:0, one launch (start us, length us, event | category | flops | bytes accessed | tf_op | source)
XLA Modules:
  0.0 275.3 jit_solution(11272264600902718)
XLA Ops:
  13.3 5.3 %all-to-all-start = ((bf16[4,8,36,1024]{3,0,2,1:T(4,128)(2,1)}), bf16[4,8,36,1024]{3,0,2,1:T(4,128)(2,1)S(1)}, u32[]{:S(2)}, u32[]{:S(2)}) async-start(bf16[4,8,36,1024]{3,0,2,1:T(4,128)(2,1)} %bitcast.37), calls=%async_computation | async-start | bytes 4718592 | tf_op jit(solution)/shard_map/all_to_all | solution.py:77
  19.0 29.1 %all-to-all-done = bf16[4,8,36,1024]{3,0,2,1:T(4,128)(2,1)S(1)} async-done(((bf16[4,8,36,1024]{3,0,2,1:T(4,128)(2,1)}), bf16[4,8,36,1024]{3,0,2,1:T(4,128)(2,1)S(1)}, u32[]{:S(2)}, u32[]{:S(2)}) %all-to-all-start) | async-done | bytes 2359328 | tf_op jit(solution)/shard_map/all_to_all | solution.py:77
  52.6 129.7 %while.17 = (s32[]{:T(128)}, bf16[8,3,12,1024]{3,0,2,1:T(8,128)(2,1)S(1)}, bf16[4,8,3,12,1024]{4,1,3,2,0:T(8,128)(2,1)}, s32[]{:T(128)}, pred[]{:T(512)}, /*inde...) while((s32[]{:T(128)}, ...), condition=%wide.region_9.10_spmd.clone, body=%wide.region_5.9_spmd.clone.sunk | while | flops 608999680 | bytes 19899208 | solution.py:96
  54.6 4.7 %conditional.3 = (bf16[8,3,12,1024]{3,2,0,1:T(8,128)(2,1)S(1)}) conditional(s32[]{:T(128)} %convert_element_type.86, bf16[8,3,12,1024]{3,2,0,1:T(8,128)(2,1)S(1)} %bitcast_select_fusion.2, (bf16[8,3,12,1024]{3,2,0,1:T(8,128)(2,1)S(1)}, f32[3]{0:T(128)S(1)}, f32[1,3,1024]{2,1,0:T(4,128)S(1)}, bf16[3,1024,1024]{2,1,0:T(8,128)(2,1)}, ...), branch_computations={%region_6.6_spmd, %region_7.8_spmd} | conditional | flops 608403712 | bytes 9269780 | solution.py:87
  62.6 8.5 %collective-permute-done = bf16[8,3,12,1024]{3,0,2,1:T(8,128)(2,1)S(1)} collective-permute-done((bf16[8,3,12,1024]{3,0,2,1:T(8,128)(2,1)S(1)}, bf16[8,3,12,1024]{3,0,2,1:T(8,128)(2,1)S(1)}, u32[]{:S(2)}, u32[]{:S(2)}) %collective-permute-start) | collective-permute-done | bytes 589856 | tf_op jit(solution)/shard_map/while/body/eval_jaxpr/ppermute | solution.py:12
  73.1 4.7 %conditional.3 = (bf16[8,3,12,1024]{3,2,0,1:T(8,128)(2,1)S(1)}) conditional(s32[]{:T(128)} %convert_element_type.86, bf16[8,3,12,1024]{3,2,0,1:T(8,128)(2,1)S(1)} %bitcast_select_fusion.2, (bf16[8,3,12,1024]{3,2,0,1:T(8,128)(2,1)S(1)}, f32[3]{0:T(128)S(1)}, f32[1,3,1024]{2,1,0:T(4,128)S(1)}, bf16[3,1024,1024]{2,1,0:T(8,128)(2,1)}, ...), branch_computations={%region_6.6_spmd, %region_7.8_spmd} | conditional | flops 608403712 | bytes 9269780 | solution.py:87
  78.2 4.4 %collective-permute-start = (bf16[8,3,12,1024]{3,0,2,1:T(8,128)(2,1)S(1)}, bf16[8,3,12,1024]{3,0,2,1:T(8,128)(2,1)S(1)}, u32[]{:S(2)}, u32[]{:S(2)}) collective-permute-start(bf16[8,3,12,1024]{3,0,2,1:T(8,128)(2,1)S(1)} %copy.66), channel_id=1, source_target_pairs={{0,8},{8,16},{16,24},{1,9},{9,17},{17,25},{2,10},{10,18},{18,26},{... | collective-permute-start | bytes 1769480 | tf_op jit(solution)/shard_map/while/body/eval_jaxpr/ppermute | solution.py:12
  84.2 7.7 %collective-permute-done = bf16[8,3,12,1024]{3,0,2,1:T(8,128)(2,1)S(1)} collective-permute-done((bf16[8,3,12,1024]{3,0,2,1:T(8,128)(2,1)S(1)}, bf16[8,3,12,1024]{3,0,2,1:T(8,128)(2,1)S(1)}, u32[]{:S(2)}, u32[]{:S(2)}) %collective-permute-start) | collective-permute-done | bytes 589856 | tf_op jit(solution)/shard_map/while/body/eval_jaxpr/ppermute | solution.py:12
  93.9 4.7 %conditional.3 = (bf16[8,3,12,1024]{3,2,0,1:T(8,128)(2,1)S(1)}) conditional(s32[]{:T(128)} %convert_element_type.86, bf16[8,3,12,1024]{3,2,0,1:T(8,128)(2,1)S(1)} %bitcast_select_fusion.2, (bf16[8,3,12,1024]{3,2,0,1:T(8,128)(2,1)S(1)}, f32[3]{0:T(128)S(1)}, f32[1,3,1024]{2,1,0:T(4,128)S(1)}, bf16[3,1024,1024]{2,1,0:T(8,128)(2,1)}, ...), branch_computations={%region_6.6_spmd, %region_7.8_spmd} | conditional | flops 608403712 | bytes 9269780 | solution.py:87
  94.3 4.3 %fusion.7 = bf16[8,3,12,1024]{3,2,0,1:T(8,128)(2,1)S(1)} fusion(bf16[8,3,12,1024]{3,2,0,1:T(8,128)(2,1)S(1)} %copy.80, bf16[3,1024,1024]{2,1,0:T(8,128)(2,1)} %get-tuple-element.218, f32[3,1024]{1,0:T(4,128)S(1)} %get-tuple-element.219, f32[3,1024]{1,0:T(4,128)S(1)} %bitcast.39, f32[8,3,12]{2,0,1:T(8,128)S(1)} %add_rsqrt_fusion), kind=kOutput, calls=%fused_computation.9 | convolution fusion | flops 607518720 | bytes 7496832 | tf_op jit(solution)/shard_map/while/body/eval_jaxpr/cond/branch_1_fun/nscd,sde->nsce/dot_general | solution.py:58
  99.0 4.4 %collective-permute-start = (bf16[8,3,12,1024]{3,0,2,1:T(8,128)(2,1)S(1)}, bf16[8,3,12,1024]{3,0,2,1:T(8,128)(2,1)S(1)}, u32[]{:S(2)}, u32[]{:S(2)}) collective-permute-start(bf16[8,3,12,1024]{3,0,2,1:T(8,128)(2,1)S(1)} %copy.66), channel_id=1, source_target_pairs={{0,8},{8,16},{16,24},{1,9},{9,17},{17,25},{2,10},{10,18},{18,26},{... | collective-permute-start | bytes 1769480 | tf_op jit(solution)/shard_map/while/body/eval_jaxpr/ppermute | solution.py:12
  104.9 6.8 %collective-permute-done = bf16[8,3,12,1024]{3,0,2,1:T(8,128)(2,1)S(1)} collective-permute-done((bf16[8,3,12,1024]{3,0,2,1:T(8,128)(2,1)S(1)}, bf16[8,3,12,1024]{3,0,2,1:T(8,128)(2,1)S(1)}, u32[]{:S(2)}, u32[]{:S(2)}) %collective-permute-start) | collective-permute-done | bytes 589856 | tf_op jit(solution)/shard_map/while/body/eval_jaxpr/ppermute | solution.py:12
  113.8 4.7 %conditional.3 = (bf16[8,3,12,1024]{3,2,0,1:T(8,128)(2,1)S(1)}) conditional(s32[]{:T(128)} %convert_element_type.86, bf16[8,3,12,1024]{3,2,0,1:T(8,128)(2,1)S(1)} %bitcast_select_fusion.2, (bf16[8,3,12,1024]{3,2,0,1:T(8,128)(2,1)S(1)}, f32[3]{0:T(128)S(1)}, f32[1,3,1024]{2,1,0:T(4,128)S(1)}, bf16[3,1024,1024]{2,1,0:T(8,128)(2,1)}, ...), branch_computations={%region_6.6_spmd, %region_7.8_spmd} | conditional | flops 608403712 | bytes 9269780 | solution.py:87
  114.2 4.3 %fusion.7 = bf16[8,3,12,1024]{3,2,0,1:T(8,128)(2,1)S(1)} fusion(bf16[8,3,12,1024]{3,2,0,1:T(8,128)(2,1)S(1)} %copy.80, bf16[3,1024,1024]{2,1,0:T(8,128)(2,1)} %get-tuple-element.218, f32[3,1024]{1,0:T(4,128)S(1)} %get-tuple-element.219, f32[3,1024]{1,0:T(4,128)S(1)} %bitcast.39, f32[8,3,12]{2,0,1:T(8,128)S(1)} %add_rsqrt_fusion), kind=kOutput, calls=%fused_computation.9 | convolution fusion | flops 607518720 | bytes 7496832 | tf_op jit(solution)/shard_map/while/body/eval_jaxpr/cond/branch_1_fun/nscd,sde->nsce/dot_general | solution.py:58
  118.9 4.4 %collective-permute-start = (bf16[8,3,12,1024]{3,0,2,1:T(8,128)(2,1)S(1)}, bf16[8,3,12,1024]{3,0,2,1:T(8,128)(2,1)S(1)}, u32[]{:S(2)}, u32[]{:S(2)}) collective-permute-start(bf16[8,3,12,1024]{3,0,2,1:T(8,128)(2,1)S(1)} %copy.66), channel_id=1, source_target_pairs={{0,8},{8,16},{16,24},{1,9},{9,17},{17,25},{2,10},{10,18},{18,26},{... | collective-permute-start | bytes 1769480 | tf_op jit(solution)/shard_map/while/body/eval_jaxpr/ppermute | solution.py:12
  124.8 6.0 %collective-permute-done = bf16[8,3,12,1024]{3,0,2,1:T(8,128)(2,1)S(1)} collective-permute-done((bf16[8,3,12,1024]{3,0,2,1:T(8,128)(2,1)S(1)}, bf16[8,3,12,1024]{3,0,2,1:T(8,128)(2,1)S(1)}, u32[]{:S(2)}, u32[]{:S(2)}) %collective-permute-start) | collective-permute-done | bytes 589856 | tf_op jit(solution)/shard_map/while/body/eval_jaxpr/ppermute | solution.py:12
  133.2 9.1 %collective-permute-start = (bf16[8,3,12,1024]{3,0,2,1:T(8,128)(2,1)S(1)}, bf16[8,3,12,1024]{3,0,2,1:T(8,128)(2,1)S(1)}, u32[]{:S(2)}, u32[]{:S(2)}) collective-permute-start(bf16[8,3,12,1024]{3,0,2,1:T(8,128)(2,1)S(1)} %copy.66), channel_id=1, source_target_pairs={{0,8},{8,16},{16,24},{1,9},{9,17},{17,25},{2,10},{10,18},{18,26},{... | collective-permute-start | bytes 1769480 | tf_op jit(solution)/shard_map/while/body/eval_jaxpr/ppermute | solution.py:12
  143.9 6.1 %collective-permute-done = bf16[8,3,12,1024]{3,0,2,1:T(8,128)(2,1)S(1)} collective-permute-done((bf16[8,3,12,1024]{3,0,2,1:T(8,128)(2,1)S(1)}, bf16[8,3,12,1024]{3,0,2,1:T(8,128)(2,1)S(1)}, u32[]{:S(2)}, u32[]{:S(2)}) %collective-permute-start) | collective-permute-done | bytes 589856 | tf_op jit(solution)/shard_map/while/body/eval_jaxpr/ppermute | solution.py:12
  152.4 4.4 %collective-permute-start = (bf16[8,3,12,1024]{3,0,2,1:T(8,128)(2,1)S(1)}, bf16[8,3,12,1024]{3,0,2,1:T(8,128)(2,1)S(1)}, u32[]{:S(2)}, u32[]{:S(2)}) collective-permute-start(bf16[8,3,12,1024]{3,0,2,1:T(8,128)(2,1)S(1)} %copy.66), channel_id=1, source_target_pairs={{0,8},{8,16},{16,24},{1,9},{9,17},{17,25},{2,10},{10,18},{18,26},{... | collective-permute-start | bytes 1769480 | tf_op jit(solution)/shard_map/while/body/eval_jaxpr/ppermute | solution.py:12
  158.4 5.8 %collective-permute-done = bf16[8,3,12,1024]{3,0,2,1:T(8,128)(2,1)S(1)} collective-permute-done((bf16[8,3,12,1024]{3,0,2,1:T(8,128)(2,1)S(1)}, bf16[8,3,12,1024]{3,0,2,1:T(8,128)(2,1)S(1)}, u32[]{:S(2)}, u32[]{:S(2)}) %collective-permute-start) | collective-permute-done | bytes 589856 | tf_op jit(solution)/shard_map/while/body/eval_jaxpr/ppermute | solution.py:12
  166.6 8.4 %collective-permute-start = (bf16[8,3,12,1024]{3,0,2,1:T(8,128)(2,1)S(1)}, bf16[8,3,12,1024]{3,0,2,1:T(8,128)(2,1)S(1)}, u32[]{:S(2)}, u32[]{:S(2)}) collective-permute-start(bf16[8,3,12,1024]{3,0,2,1:T(8,128)(2,1)S(1)} %copy.66), channel_id=1, source_target_pairs={{0,8},{8,16},{16,24},{1,9},{9,17},{17,25},{2,10},{10,18},{18,26},{... | collective-permute-start | bytes 1769480 | tf_op jit(solution)/shard_map/while/body/eval_jaxpr/ppermute | solution.py:12
  176.5 5.8 %collective-permute-done = bf16[8,3,12,1024]{3,0,2,1:T(8,128)(2,1)S(1)} collective-permute-done((bf16[8,3,12,1024]{3,0,2,1:T(8,128)(2,1)S(1)}, bf16[8,3,12,1024]{3,0,2,1:T(8,128)(2,1)S(1)}, u32[]{:S(2)}, u32[]{:S(2)}) %collective-permute-start) | collective-permute-done | bytes 589856 | tf_op jit(solution)/shard_map/while/body/eval_jaxpr/ppermute | solution.py:12
  185.8 46.8 %all_to_all.10 = bf16[4,8,36,1024]{3,0,2,1:T(4,128)(2,1)S(1)} all-to-all(bf16[4,8,36,1024]{3,0,2,1:T(4,128)(2,1)S(1)} %copy.41), channel_id=1, replica_groups=mesh['section'=4,'rep'=8] {'rep'}, dimensions={1} | all-to-all | bytes 4718592 | tf_op jit(solution)/shard_map/all_to_all | solution.py:97
  235.3 33.2 %reduce-scatter.2.cloned.1.call-done = bf16[4,128,256]{2,1,0:T(8,128)(2,1)} async-done(((bf16[4,128,1024]{2,1,0:T(8,128)(2,1)}), bf16[4,128,256]{2,1,0:T(8,128)(2,1)}) %reduce-scatter.2.cloned.1.call-update) | async-done | bytes 262160 | tf_op jit(solution)/shard_map/reduce_scatter | solution.py:111
  (84 shorter events, 56.3 us)
Async XLA Ops:
  13.3 5.4 %copy-start = (f32[1,3,1024]{2,0,1:T(1,128)S(1)}, f32[1,3,1024]{2,0,1:T(1,128)}, u32[]{:S(2)}) copy-start(f32[1,3,1024]{2,0,1:T(1,128)} %param.14) | copy-start | bytes 36868
  13.3 5.4 %copy-start.1 = (s32[16]{0:T(128)S(1)}, s32[16]{0:T(128)}, u32[]{:S(2)}) copy-start(s32[16]{0:T(128)} %param.13) | copy-start | bytes 196
  13.3 5.4 %copy-start.2 = (s32[16]{0:T(128)S(1)}, s32[16]{0:T(128)}, u32[]{:S(2)}) copy-start(s32[16]{0:T(128)} %param.12) | copy-start | bytes 196
  13.3 34.8 %all-to-all-start = ((bf16[4,8,36,1024]{3,0,2,1:T(4,128)(2,1)}), bf16[4,8,36,1024]{3,0,2,1:T(4,128)(2,1)S(1)}, u32[]{:S(2)}, u32[]{:S(2)}) async-start(bf16[4,8,36,1024]{3,0,2,1:T(4,128)(2,1)} %bitcast.37), calls=%async_computation | async-start | bytes 4718592 | tf_op jit(solution)/shard_map/all_to_all | solution.py:77
  18.7 249.7 %reduce-scatter.2.cloned.1.call-start = ((), (), s32[]{:S(2)}) async-start(), calls=%async_computation.3 | async-start | bytes 1310720 | tf_op jit(solution)/shard_map/reduce_scatter | solution.py:111
  59.7 11.4 %collective-permute-start = (bf16[8,3,12,1024]{3,0,2,1:T(8,128)(2,1)S(1)}, bf16[8,3,12,1024]{3,0,2,1:T(8,128)(2,1)S(1)}, u32[]{:S(2)}, u32[]{:S(2)}) collective-permute-start(bf16[8,3,12,1024]{3,0,2,1:T(8,128)(2,1)S(1)} %copy.66), channel_id=1, source_target_pairs={{0,8},{8,16},{16,24},{1,9},{9,17},{17,25},{2,10},{10,18},{18,26},{... | collective-permute-start | bytes 1769480 | tf_op jit(solution)/shard_map/while/body/eval_jaxpr/ppermute | solution.py:12
  78.2 13.6 %collective-permute-start = (bf16[8,3,12,1024]{3,0,2,1:T(8,128)(2,1)S(1)}, bf16[8,3,12,1024]{3,0,2,1:T(8,128)(2,1)S(1)}, u32[]{:S(2)}, u32[]{:S(2)}) collective-permute-start(bf16[8,3,12,1024]{3,0,2,1:T(8,128)(2,1)S(1)} %copy.66), channel_id=1, source_target_pairs={{0,8},{8,16},{16,24},{1,9},{9,17},{17,25},{2,10},{10,18},{18,26},{... | collective-permute-start | bytes 1769480 | tf_op jit(solution)/shard_map/while/body/eval_jaxpr/ppermute | solution.py:12
  99.0 12.8 %collective-permute-start = (bf16[8,3,12,1024]{3,0,2,1:T(8,128)(2,1)S(1)}, bf16[8,3,12,1024]{3,0,2,1:T(8,128)(2,1)S(1)}, u32[]{:S(2)}, u32[]{:S(2)}) collective-permute-start(bf16[8,3,12,1024]{3,0,2,1:T(8,128)(2,1)S(1)} %copy.66), channel_id=1, source_target_pairs={{0,8},{8,16},{16,24},{1,9},{9,17},{17,25},{2,10},{10,18},{18,26},{... | collective-permute-start | bytes 1769480 | tf_op jit(solution)/shard_map/while/body/eval_jaxpr/ppermute | solution.py:12
  118.9 11.9 %collective-permute-start = (bf16[8,3,12,1024]{3,0,2,1:T(8,128)(2,1)S(1)}, bf16[8,3,12,1024]{3,0,2,1:T(8,128)(2,1)S(1)}, u32[]{:S(2)}, u32[]{:S(2)}) collective-permute-start(bf16[8,3,12,1024]{3,0,2,1:T(8,128)(2,1)S(1)} %copy.66), channel_id=1, source_target_pairs={{0,8},{8,16},{16,24},{1,9},{9,17},{17,25},{2,10},{10,18},{18,26},{... | collective-permute-start | bytes 1769480 | tf_op jit(solution)/shard_map/while/body/eval_jaxpr/ppermute | solution.py:12
  133.2 16.8 %collective-permute-start = (bf16[8,3,12,1024]{3,0,2,1:T(8,128)(2,1)S(1)}, bf16[8,3,12,1024]{3,0,2,1:T(8,128)(2,1)S(1)}, u32[]{:S(2)}, u32[]{:S(2)}) collective-permute-start(bf16[8,3,12,1024]{3,0,2,1:T(8,128)(2,1)S(1)} %copy.66), channel_id=1, source_target_pairs={{0,8},{8,16},{16,24},{1,9},{9,17},{17,25},{2,10},{10,18},{18,26},{... | collective-permute-start | bytes 1769480 | tf_op jit(solution)/shard_map/while/body/eval_jaxpr/ppermute | solution.py:12
  152.4 11.8 %collective-permute-start = (bf16[8,3,12,1024]{3,0,2,1:T(8,128)(2,1)S(1)}, bf16[8,3,12,1024]{3,0,2,1:T(8,128)(2,1)S(1)}, u32[]{:S(2)}, u32[]{:S(2)}) collective-permute-start(bf16[8,3,12,1024]{3,0,2,1:T(8,128)(2,1)S(1)} %copy.66), channel_id=1, source_target_pairs={{0,8},{8,16},{16,24},{1,9},{9,17},{17,25},{2,10},{10,18},{18,26},{... | collective-permute-start | bytes 1769480 | tf_op jit(solution)/shard_map/while/body/eval_jaxpr/ppermute | solution.py:12
  166.6 15.7 %collective-permute-start = (bf16[8,3,12,1024]{3,0,2,1:T(8,128)(2,1)S(1)}, bf16[8,3,12,1024]{3,0,2,1:T(8,128)(2,1)S(1)}, u32[]{:S(2)}, u32[]{:S(2)}) collective-permute-start(bf16[8,3,12,1024]{3,0,2,1:T(8,128)(2,1)S(1)} %copy.66), channel_id=1, source_target_pairs={{0,8},{8,16},{16,24},{1,9},{9,17},{17,25},{2,10},{10,18},{18,26},{... | collective-permute-start | bytes 1769480 | tf_op jit(solution)/shard_map/while/body/eval_jaxpr/ppermute | solution.py:12
Sparse Core Ops, SparseCore 0:
  235.4 32.9 reduce-scatter.1
where the time goes:
time: 276 us; the launch traced here: 275 us
  waiting for transfers between devices  109 us (39%)
  blocking collectives  46.8 us (17%)
  starting transfers between devices  41.9 us (15%)
  local copies, waits for them, and re-layouts  31.1 us (11%)
  matrix products  22 us (8%)
  between operations  13.5 us (5%)
  other arithmetic  10.4 us (4%)
    all_to_all x1, blocking collectives, on_device(): lax.all_to_all(slot_results.reshape(batches, rep_count, slot_count * capa...  46.8 us
    ppermute x7, waiting for transfers between devices, shifted(): return lax.ppermute(x, axis, pairs)  46.8 us
    ppermute x7, starting transfers between devices, shifted(): return lax.ppermute(x, axis, pairs)  36.5 us
    reduce_scatter x1, waiting for transfers between devices, on_device(): lax.psum_scatter(contribution.astype(jnp.bfloat16), 'section', scatter_di...  33.2 us
    all_to_all x1, waiting for transfers between devices, on_device(): lax.all_to_all(outgoing, 'rep', split_axis=1, concat_axis=1, tiled=True)  29.1 us
    select_n x14, local copies, waits for them, and re-layouts, tick(): outbuf = jnp.where(storing, stored, outbuf)  17.3 us
    dot_general x4, matrix products, update(): jnp.einsum('nscd,sde->nsce', lowered, section_weight, preferred_element_t...  17.3 us
  transfers between devices with their start and end apart: 9, of which 9 were waited for; matrix products, arithmetic and copies ran while one was open for 4% of the time, Pallas kernels for 0%

commit v1 on v0

v1 whole, which is shorter than its diff:
```python
import functools
import jax
import jax.numpy as jnp
from jax import lax
from jax.experimental import pallas as pl
from jax.experimental.pallas import tpu as pltpu
from jax.sharding import PartitionSpec as P

epsilon = 1e-05
STREAMS = 2
VMEM_LIMIT = 40 * 1024 * 1024


def earlier_same(first, second, at):
    rows = lax.broadcasted_iota(jnp.int32, (first.shape[0], second.shape[1]), 0)
    lanes = lax.broadcasted_iota(jnp.int32, (first.shape[0], second.shape[1]), 1)
    before = rows < lanes if at == 1 else lanes < rows
    return jnp.where((first == second) & before, 1, 0)


def targets(ids, other, at, table, batch, capacity):
    position = jnp.sum(
        earlier_same(other, ids, 1) if at == 1 else earlier_same(ids, other, 0),
        axis=0 if at == 1 else 1,
        keepdims=True,
    )
    base = jnp.zeros_like(ids)
    for replica, start in enumerate(table):
        base = jnp.where(ids == replica, start, base)
    return base + position + batch * capacity


def start_table(placement, me, slot_count, batches, capacity):
    slot_rows = batches * capacity
    found = []
    for replica in range(placement.shape[0]):
        slot = placement[replica]
        holder = lax.div(slot, slot_count)
        within = slot - holder * slot_count
        found.append((holder ^ me) * (slot_count * slot_rows) + within * slot_rows)
    return found


def dispatch_kernel(sizes, me, placement, lane_ids, row_ids, tokens, *chunks):
    batches, row_count, slot_count, capacity = sizes
    table = start_table(placement, me[0], slot_count, batches, capacity)
    target = jnp.concatenate(
        [
            targets(lane_ids[m], row_ids[m], 1, table, m, capacity)
            for m in range(batches)
        ],
        axis=1,
    )
    slot_rows = batches * capacity
    chunk_rows = slot_count * slot_rows
    source = jnp.concatenate([tokens[m] for m in range(batches)], axis=0)
    for i, chunk in enumerate(chunks):
        wanted = lax.broadcasted_iota(jnp.int32, (chunk_rows, batches * row_count), 0)
        picked = jnp.where(target == wanted + i * chunk_rows, 1.0, 0.0).astype(jnp.bfloat16)
        moved = jnp.dot(picked, source, preferred_element_type=jnp.float32).astype(jnp.bfloat16)
        for j in range(slot_count):
            chunk[j] = moved[j * slot_rows : (j + 1) * slot_rows]


def combine_kernel(sizes, me, placement, lane_ids, row_ids, returned, out):
    batches, row_count, slot_count, capacity = sizes
    table = start_table(placement, me[0], slot_count, batches, capacity)
    chunk_count = returned.shape[0]
    flat = jnp.concatenate(
        [returned[i, j] for i in range(chunk_count) for j in range(slot_count)], axis=0
    )
    for m in range(batches):
        target = targets(row_ids[m], lane_ids[m], 0, table, m, capacity)
        held = lax.broadcasted_iota(jnp.int32, (row_count, flat.shape[0]), 1)
        picked = jnp.where(target == held, 1.0, 0.0).astype(jnp.bfloat16)
        out[m] = jnp.dot(picked, flat, preferred_element_type=jnp.float32).astype(jnp.bfloat16)


def layer_kernel(two, is_first, width, scale, *refs):
    if two:
        first, arrived, gain, weight, out = refs
        rows = jnp.where(is_first[0] == 1, first[0], arrived[0]).astype(jnp.float32)
    else:
        arrived, gain, weight, out = refs
        rows = arrived[0].astype(jnp.float32)
    slot = pl.program_id(0)
    live = lax.broadcasted_iota(jnp.int32, (1, rows.shape[1]), 1) < width[slot]
    rows = jnp.where(live, rows, 0.0)
    mean_square = jnp.sum(rows * rows, axis=1, keepdims=True) * scale[slot]
    lowered = (rows * lax.rsqrt(mean_square + epsilon) * gain[0]).astype(jnp.bfloat16)
    projected = jnp.dot(lowered, weight[0], preferred_element_type=jnp.float32)
    gate = projected * jax.nn.sigmoid(projected)
    out[0] = (rows + jnp.where(live, gate, 0.0)).astype(jnp.bfloat16)


def layer(first, arrived, is_first, width, scale, gain, weight):
    given = [a for a in (first, arrived) if a is not None]
    slot_count, slot_rows, depth = given[0].shape
    smem = pl.BlockSpec(memory_space=pltpu.SMEM)
    block = pl.BlockSpec((1, slot_rows, depth), lambda j: (j, 0, 0))
    return pl.pallas_call(
        functools.partial(layer_kernel, len(given) == 2),
        grid=(slot_count,),
        in_specs=[smem] * 3
        + [block] * len(given)
        + [
            pl.BlockSpec((1, 1, depth), lambda j: (j, 0, 0)),
            pl.BlockSpec((1, depth, depth), lambda j: (j, 0, 0)),
        ],
        out_specs=block,
        out_shape=jax.ShapeDtypeStruct(given[0].shape, jnp.bfloat16),
        compiler_params=pltpu.CompilerParams(vmem_limit_bytes=VMEM_LIMIT),
        cost_estimate=pl.CostEstimate(
            flops=2 * slot_count * slot_rows * depth * depth,
            bytes_accessed=2 * slot_count * depth * (depth + 3 * slot_rows),
            transcendentals=0,
        ),
        name="layer",
    )(is_first, width, scale, *given, gain, weight)


def on_device(tokens, replica_of_row, widths, placement, gains, weights):
    batches, row_count, depth = tokens.shape
    rep_count = lax.axis_size("rep")
    section_count = lax.axis_size("section")
    slot_count = weights.shape[1]
    replica_count = widths.shape[0]
    capacity = (3 * row_count + 2 * replica_count - 1) // (2 * replica_count)
    section_id = lax.axis_index("section")
    rep_id = lax.axis_index("rep")
    last = section_count - 1
    part = depth // section_count
    slot_rows = batches * capacity

    global_ids = rep_id * slot_count + jnp.arange(slot_count, dtype=jnp.int32)
    width = jnp.sum(
        jnp.where(placement[None, :] == global_ids[:, None], widths[None, :], 0), axis=1
    )
    scale = 1.0 / jnp.maximum(width, 1).astype(jnp.float32)
    is_first = (section_id == 0).astype(jnp.int32).reshape(1)
    me = rep_id.astype(jnp.int32).reshape(1)
    gain = gains.reshape(slot_count, 1, depth)
    weight = weights.reshape(slot_count, depth, depth)
    lane_ids = replica_of_row.reshape(batches, 1, row_count)

    sizes = (batches, row_count, slot_count, capacity)
    smem = pl.BlockSpec(memory_space=pltpu.SMEM)
    vmem = pl.BlockSpec(memory_space=pltpu.VMEM)
    chunk_shape = jax.ShapeDtypeStruct((slot_count, slot_rows, depth), jnp.bfloat16)
    outgoing = pl.pallas_call(
        functools.partial(dispatch_kernel, sizes),
        in_specs=[smem, smem, vmem, vmem, vmem],
        out_specs=[vmem] * rep_count,
        out_shape=[chunk_shape] * rep_count,
        compiler_params=pltpu.CompilerParams(vmem_limit_bytes=VMEM_LIMIT),
        name="dispatch",
    )(me, placement, lane_ids, replica_of_row, tokens)

    def traded(x, i):
        if i == 0:
            return x
        return lax.ppermute(x, "rep", [(d, d ^ i) for d in range(rep_count)])

    entering = [traded(outgoing[i], i) for i in range(rep_count)]
    forward = [(s, s + 1) for s in range(last)]
    lag = STREAMS * last
    inbound, finished = {}, []
    for n in range(rep_count + lag):
        first = entering[n] if n < rep_count else None
        arrived = inbound.get(n)
        done = layer(first, arrived, is_first, width, scale, gain, weight)
        if n < rep_count + lag - STREAMS:
            inbound[n + STREAMS] = lax.ppermute(done, "section", forward)
        if n >= lag:
            finished.append(done)

    half, quarter = rep_count // 2, rep_count // 4
    pieces = []
    for low, high in ((0, half), (half, half + quarter), (half + quarter, rep_count)):
        group = jnp.stack(finished[low:high])
        mine = group[..., last * part :]
        for s in range(last):
            sent = lax.ppermute(group[..., s * part : (s + 1) * part], "section", [(last, s)])
            mine = jnp.where(section_id == s, sent, mine)
        pieces.append(mine)
    held = jnp.concatenate(pieces)
    by_owner = jnp.stack(
        [lax.dynamic_index_in_dim(held, rep_id ^ b, 0, keepdims=False) for b in range(rep_count)]
    )
    returned = lax.all_to_all(by_owner, "rep", split_axis=0, concat_axis=0, tiled=True)
    zero = jnp.zeros((1,), jnp.int32)
    return pl.pallas_call(
        functools.partial(combine_kernel, sizes),
        in_specs=[smem, smem, vmem, vmem, vmem],
        out_specs=vmem,
        out_shape=jax.ShapeDtypeStruct((batches, row_count, part), jnp.bfloat16),
        compiler_params=pltpu.CompilerParams(vmem_limit_bytes=VMEM_LIMIT),
        name="combine",
    )(zero, placement, lane_ids, replica_of_row, returned)


def solution(mesh):
    placed = (
        P(None, "rep", None),
        P(None, "rep", None),
        P(),
        P(),
        P("section", "rep", None),
        P("section", "rep", None, None),
    )
    return jax.shard_map(
        on_device, mesh=mesh, in_specs=placed, out_specs=P(None, "rep", "section"), check_vma=False
    )
```

time: 276 us -> 147 us (0.53)
  waiting for transfers between devices: 109 us -> 19.1 us
  Pallas kernels: 0 us -> 36.6 us
  blocking collectives: 46.8 us -> 15.1 us
  starting transfers between devices: 41.9 us -> 64.2 us
  matrix products: 22 us -> 0 us
  local copies, waits for them, and re-layouts: 31.1 us -> 9.19 us
  between operations: 13.5 us -> 0.63 us
  other arithmetic: 10.4 us -> 1.73 us
    pallas_call x0 -> x16, Pallas kernels: none -> 36.6 us  [the longest x14 32.3 us: layer(): pl.pallas_call(functools.partial(layer_kernel, len(given) == 2), grid=(sl...]
    reduce_scatter x1 -> x0, waiting for transfers between devices: 33.2 us -> none  [on_device(): lax.psum_scatter(contribution.astype(jnp.bfloat16), 'section', scatter_di...]
    all_to_all x1, blocking collectives: 46.8 us -> 15.1 us  [on_device(): lax.all_to_all(by_owner, 'rep', split_axis=0, concat_axis=0, tiled=True)]
    all_to_all x1 -> x0, waiting for transfers between devices: 29.1 us -> none  [on_device(): lax.all_to_all(outgoing, 'rep', split_axis=1, concat_axis=1, tiled=True)]
    ppermute x7 -> x28, waiting for transfers between devices: 46.8 us -> 19.1 us  [the longest x9 13.1 us: on_device(): lax.ppermute(group[..., s * part:(s + 1) * part], 'section', [(last, s)])]
    ppermute x7 -> x28, starting transfers between devices: 36.5 us -> 64.2 us  [the longest x12 46.1 us: on_device(): inbound[n + STREAMS] = lax.ppermute(done, 'section', forward)]
    dot_general x6 -> x0, matrix products: 22 us -> none  [the longest x4 17.3 us: update(): jnp.einsum('nscd,sde->nsce', lowered, section_weight, preferred_element_t...]
    select_n x14 -> x0, local copies, waits for them, and re-layouts: 17.3 us -> none  [tick(): outbuf = jnp.where(storing, stored, outbuf)]
  transfers between devices with their start and end apart: 9 -> 28, of which waited for: 9 -> 7; matrix products, arithmetic and copies ran while one was open for 4% -> 1% of each run, Pallas kernels for 0% -> 22%
where the time goes in v1:
time: 147 us
  starting transfers between devices  64.2 us (44%)
  Pallas kernels  36.6 us (25%)
  waiting for transfers between devices  19.1 us (13%)
  blocking collectives  15.1 us (10%)
  local copies, waits for them, and re-layouts  9.19 us (6%)
  other arithmetic  1.73 us (1%)
    ppermute x12, starting transfers between devices, on_device(): inbound[n + STREAMS] = lax.ppermute(done, 'section', forward)  46.1 us
    pallas_call x14, Pallas kernels, layer(): pl.pallas_call(functools.partial(layer_kernel, len(given) == 2), grid=(sl...  32.3 us
    all_to_all x1, blocking collectives, on_device(): lax.all_to_all(by_owner, 'rep', split_axis=0, concat_axis=0, tiled=True)  15.1 us
    ppermute x9, waiting for transfers between devices, on_device(): lax.ppermute(group[..., s * part:(s + 1) * part], 'section', [(last, s)])  13.1 us
    ppermute x9, starting transfers between devices, on_device(): lax.ppermute(group[..., s * part:(s + 1) * part], 'section', [(last, s)])  9.29 us
    unnamed x28, local copies, waits for them, and re-layouts  9.1 us
    ppermute x7, starting transfers between devices, traded(): return lax.ppermute(x, 'rep', [(d, d ^ i) for d in range(rep_count)])  8.76 us
    ppermute x12, waiting for transfers between devices, on_device(): inbound[n + STREAMS] = lax.ppermute(done, 'section', forward)  6.01 us
  transfers between devices with their start and end apart: 28, of which 7 were waited for; matrix products, arithmetic and copies ran while one was open for 1% of the time, Pallas kernels for 22%

profile of v1, /device:TPU:0, one launch (start us, length us, event | category | flops | bytes accessed | tf_op | source)
XLA Modules:
  0.0 146.6 jit_solution(13560176407465828095)
XLA Ops:
  5.6 3.0 %collective-permute-start.2 = (bf16[3,48,1024]{2,1,0:T(8,128)(2,1)S(1)}, bf16[3,48,1024]{2,1,0:T(8,128)(2,1)S(1)}, u32[]{:S(2)}, u32[]{:S(2)}) collective-permute-start(bf16[3,48,1024]{2,1,0:T(8,128)(2,1)S(1)} %get-tuple-element.15), channel_id=1, source_target_pairs={{0,2},{1,3},{2,0},{3,1},{4,6},{5,7},{6,4},{7,5},{8,10},{9,11},{10,... | collective-permute-start | bytes 884744 | tf_op jit(solution)/shard_map/ppermute | solution.py:162
  8.8 2.8 %copy-done = bf16[1,3,1024,1024]{3,2,1,0:T(8,128)(2,1)S(1)} copy-done((bf16[1,3,1024,1024]{3,2,1,0:T(8,128)(2,1)S(1)}, bf16[1,3,1024,1024]{3,2,1,0:T(8,128)(2,1)}, u32[]{:S(2)}) %copy-start) | copy-done | bytes 6291480
  13.8 3.5 %collective-permute-start.3 = (bf16[3,48,1024]{2,1,0:T(8,128)(2,1)S(1)}, bf16[3,48,1024]{2,1,0:T(8,128)(2,1)S(1)}, u32[]{:S(2)}, u32[]{:S(2)}) collective-permute-start(bf16[3,48,1024]{2,1,0:T(8,128)(2,1)S(1)} %layer.14), channel_id=1, source_target_pairs={{0,8},{8,16},{16,24},{1,9},{9,17},{17,25},{2,10},{10,18},{18,26},{... | collective-permute-start | bytes 884744 | tf_op jit(solution)/shard_map/ppermute | solution.py:173
  19.0 4.3 %collective-permute-done.3.refs_1_ = bf16[3,48,1024]{2,1,0:T(8,128)(2,1)S(1)} collective-permute-done((bf16[3,48,1024]{2,1,0:T(8,128)(2,1)S(1)}, bf16[3,48,1024]{2,1,0:T(8,128)(2,1)S(1)}, u32[]{:S(2)}, u32[]{:S(2)}) %collective-permute-start.3) | collective-permute-done | bytes 294944 | tf_op jit(solution)/shard_map/ppermute | solution.py:173
  25.6 4.4 %collective-permute-start.4 = (bf16[3,48,1024]{2,1,0:T(8,128)(2,1)S(1)}, bf16[3,48,1024]{2,1,0:T(8,128)(2,1)S(1)}, u32[]{:S(2)}, u32[]{:S(2)}) collective-permute-start(bf16[3,48,1024]{2,1,0:T(8,128)(2,1)S(1)} %layer.15), channel_id=1, source_target_pairs={{0,8},{8,16},{16,24},{1,9},{9,17},{17,25},{2,10},{10,18},{18,26},{... | collective-permute-start | bytes 884744 | tf_op jit(solution)/shard_map/ppermute | solution.py:173
  30.1 2.3 %layer.18 = bf16[3,48,1024]{2,1,0:T(8,128)(2,1)S(1)} custom-call(s32[1]{0:T(128)} %bitcast.1.is_first, s32[3]{0:T(128)S(1)} %select_reduce_fusion.width, f32[3]{0:T(128)S(1)} %convert_divide_fusion.scale, bf16[3,48,1024]{2,1,0:T(8,128)(2,1)S(1)} %collective-permute-done.9.refs_0_, f32[3,1,1024]{2,1,0:T(1,128)S(1)} %bitcast.37, ...), custom_call_target="tpu_custom_call" | custom-call | flops 301989888 | bytes 7176192 | tf_op jit(solution)/shard_map/layer/pallas_call | solution.py:101
  32.4 3.5 %collective-permute-start.10 = (bf16[3,48,1024]{2,1,0:T(8,128)(2,1)S(1)}, bf16[3,48,1024]{2,1,0:T(8,128)(2,1)S(1)}, u32[]{:S(2)}, u32[]{:S(2)}) collective-permute-start(bf16[3,48,1024]{2,1,0:T(8,128)(2,1)S(1)} %layer.18), channel_id=1, source_target_pairs={{0,8},{8,16},{16,24},{1,9},{9,17},{17,25},{2,10},{10,18},{18,26},{... | collective-permute-start | bytes 884744 | tf_op jit(solution)/shard_map/ppermute | solution.py:173
  41.0 3.5 %collective-permute-start.5 = (bf16[3,48,1024]{2,1,0:T(8,128)(2,1)S(1)}, bf16[3,48,1024]{2,1,0:T(8,128)(2,1)S(1)}, u32[]{:S(2)}, u32[]{:S(2)}) collective-permute-start(bf16[3,48,1024]{2,1,0:T(8,128)(2,1)S(1)} %layer.16), channel_id=1, source_target_pairs={{0,8},{8,16},{16,24},{1,9},{9,17},{17,25},{2,10},{10,18},{18,26},{... | collective-permute-start | bytes 884744 | tf_op jit(solution)/shard_map/ppermute | solution.py:173
  44.5 2.3 %layer.19 = bf16[3,48,1024]{2,1,0:T(8,128)(2,1)S(1)} custom-call(s32[1]{0:T(128)} %bitcast.1.is_first, s32[3]{0:T(128)S(1)} %select_reduce_fusion.width, f32[3]{0:T(128)S(1)} %convert_divide_fusion.scale, bf16[3,48,1024]{2,1,0:T(8,128)(2,1)S(1)} %collective-permute-done.8.refs_0_, bf16[3,48,1024]{2,1,0:T(8,128)(2,1)S(1)} %collective-permute-done.10.refs_1_, ...), custom_call_target="tpu_custom_call" | custom-call | flops 301989888 | bytes 7176192 | tf_op jit(solution)/shard_map/layer/pallas_call | solution.py:101
  46.8 2.9 %collective-permute-start.11 = (bf16[3,48,1024]{2,1,0:T(8,128)(2,1)S(1)}, bf16[3,48,1024]{2,1,0:T(8,128)(2,1)S(1)}, u32[]{:S(2)}, u32[]{:S(2)}) collective-permute-start(bf16[3,48,1024]{2,1,0:T(8,128)(2,1)S(1)} %layer.19), channel_id=1, source_target_pairs={{0,8},{8,16},{16,24},{1,9},{9,17},{17,25},{2,10},{10,18},{18,26},{... | collective-permute-start | bytes 884744 | tf_op jit(solution)/shard_map/ppermute | solution.py:173
  54.1 4.4 %collective-permute-start.13 = (bf16[3,48,1024]{2,1,0:T(8,128)(2,1)S(1)}, bf16[3,48,1024]{2,1,0:T(8,128)(2,1)S(1)}, u32[]{:S(2)}, u32[]{:S(2)}) collective-permute-start(bf16[3,48,1024]{2,1,0:T(8,128)(2,1)S(1)} %layer.17), channel_id=1, source_target_pairs={{0,8},{8,16},{16,24},{1,9},{9,17},{17,25},{2,10},{10,18},{18,26},{... | collective-permute-start | bytes 884744 | tf_op jit(solution)/shard_map/ppermute | solution.py:173
  58.6 2.3 %layer.20 = bf16[3,48,1024]{2,1,0:T(8,128)(2,1)S(1)} custom-call(s32[1]{0:T(128)} %bitcast.1.is_first, s32[3]{0:T(128)S(1)} %select_reduce_fusion.width, f32[3]{0:T(128)S(1)} %convert_divide_fusion.scale, bf16[3,48,1024]{2,1,0:T(8,128)(2,1)S(1)} %collective-permute-done.7.refs_0_, bf16[3,48,1024]{2,1,0:T(8,128)(2,1)S(1)} %collective-permute-done.11.refs_1_, ...), custom_call_target="tpu_custom_call" | custom-call | flops 301989888 | bytes 7176192 | tf_op jit(solution)/shard_map/layer/pallas_call | solution.py:101
  60.9 3.0 %collective-permute-start.12 = (bf16[3,48,1024]{2,1,0:T(8,128)(2,1)S(1)}, bf16[3,48,1024]{2,1,0:T(8,128)(2,1)S(1)}, u32[]{:S(2)}, u32[]{:S(2)}) collective-permute-start(bf16[3,48,1024]{2,1,0:T(8,128)(2,1)S(1)} %layer.20), channel_id=1, source_target_pairs={{0,8},{8,16},{16,24},{1,9},{9,17},{17,25},{2,10},{10,18},{18,26},{... | collective-permute-start | bytes 884744 | tf_op jit(solution)/shard_map/ppermute | solution.py:173
  63.9 2.3 %layer.22 = bf16[3,48,1024]{2,1,0:T(8,128)(2,1)S(1)} custom-call(s32[1]{0:T(128)} %bitcast.1.is_first, s32[3]{0:T(128)S(1)} %select_reduce_fusion.width, f32[3]{0:T(128)S(1)} %convert_divide_fusion.scale, bf16[3,48,1024]{2,1,0:T(8,128)(2,1)S(1)} %collective-permute-done.13.refs_0_, f32[3,1,1024]{2,1,0:T(1,128)S(1)} %bitcast.42, ...), custom_call_target="tpu_custom_call" | custom-call | flops 301989888 | bytes 7176192 | tf_op jit(solution)/shard_map/layer/pallas_call | solution.py:101
  66.2 4.4 %collective-permute-start.18 = (bf16[3,48,1024]{2,1,0:T(8,128)(2,1)S(1)}, bf16[3,48,1024]{2,1,0:T(8,128)(2,1)S(1)}, u32[]{:S(2)}, u32[]{:S(2)}) collective-permute-start(bf16[3,48,1024]{2,1,0:T(8,128)(2,1)S(1)} %layer.22), channel_id=1, source_target_pairs={{0,8},{8,16},{16,24},{1,9},{9,17},{17,25},{2,10},{10,18},{18,26},{... | collective-permute-start | bytes 884744 | tf_op jit(solution)/shard_map/ppermute | solution.py:173
  73.5 4.4 %collective-permute-start.14 = (bf16[3,48,1024]{2,1,0:T(8,128)(2,1)S(1)}, bf16[3,48,1024]{2,1,0:T(8,128)(2,1)S(1)}, u32[]{:S(2)}, u32[]{:S(2)}) collective-permute-start(bf16[3,48,1024]{2,1,0:T(8,128)(2,1)S(1)} %layer.21), channel_id=1, source_target_pairs={{0,8},{8,16},{16,24},{1,9},{9,17},{17,25},{2,10},{10,18},{18,26},{... | collective-permute-start | bytes 884744 | tf_op jit(solution)/shard_map/ppermute | solution.py:173
  80.3 3.4 %collective-permute-start.23 = (bf16[3,48,1024]{2,1,0:T(8,128)(2,1)S(1)}, bf16[3,48,1024]{2,1,0:T(8,128)(2,1)S(1)}, u32[]{:S(2)}, u32[]{:S(2)}) collective-permute-start(bf16[3,48,1024]{2,1,0:T(8,128)(2,1)S(1)} %layer.24), channel_id=1, source_target_pairs={{0,8},{8,16},{16,24},{1,9},{9,17},{17,25},{2,10},{10,18},{18,26},{... | collective-permute-start | bytes 884744 | tf_op jit(solution)/shard_map/ppermute | solution.py:173
  86.0 4.4 %collective-permute-start.19 = (bf16[3,48,1024]{2,1,0:T(8,128)(2,1)S(1)}, bf16[3,48,1024]{2,1,0:T(8,128)(2,1)S(1)}, u32[]{:S(2)}, u32[]{:S(2)}) collective-permute-start(bf16[3,48,1024]{2,1,0:T(8,128)(2,1)S(1)} %layer.23), channel_id=1, source_target_pairs={{0,8},{8,16},{16,24},{1,9},{9,17},{17,25},{2,10},{10,18},{18,26},{... | collective-permute-start | bytes 884744 | tf_op jit(solution)/shard_map/ppermute | solution.py:173
  95.0 2.8 %copy-done.2 = bf16[1,3,1024,1024]{3,2,1,0:T(8,128)(2,1)S(1)} copy-done((bf16[1,3,1024,1024]{3,2,1,0:T(8,128)(2,1)S(1)}, bf16[1,3,1024,1024]{3,2,1,0:T(8,128)(2,1)}, u32[]{:S(2)}) %copy-start.2) | copy-done | bytes 6291480
  100.1 4.4 %collective-permute-start.24 = (bf16[3,48,1024]{2,1,0:T(8,128)(2,1)S(1)}, bf16[3,48,1024]{2,1,0:T(8,128)(2,1)S(1)}, u32[]{:S(2)}, u32[]{:S(2)}) collective-permute-start(bf16[3,48,1024]{2,1,0:T(8,128)(2,1)S(1)} %layer.25), channel_id=1, source_target_pairs={{0,8},{8,16},{16,24},{1,9},{9,17},{17,25},{2,10},{10,18},{18,26},{... | collective-permute-start | bytes 884744 | tf_op jit(solution)/shard_map/ppermute | solution.py:173
  109.5 3.5 %collective-permute-done.17 = bf16[4,3,48,256]{3,2,1,0:T(8,128)(2,1)} collective-permute-done((bf16[4,3,48,256]{3,2,1,0:T(8,128)(2,1)S(1)}, bf16[4,3,48,256]{3,2,1,0:T(8,128)(2,1)}, u32[]{:S(2)}, u32[]{:S(2)}) %collective-permute-start.17) | collective-permute-done | bytes 294944 | tf_op jit(solution)/shard_map/ppermute | solution.py:183
  119.2 3.3 %collective-permute-done.22 = bf16[2,3,48,256]{3,2,1,0:T(8,128)(2,1)S(1)} collective-permute-done((bf16[2,3,48,256]{3,2,1,0:T(8,128)(2,1)S(1)}, bf16[2,3,48,256]{3,2,1,0:T(8,128)(2,1)S(1)}, u32[]{:S(2)}, u32[]{:S(2)}) %collective-permute-start.22) | collective-permute-done | bytes 147488 | tf_op jit(solution)/shard_map/ppermute | solution.py:183
  122.6 6.3 %collective-permute-done.27 = bf16[2,3,48,256]{3,2,1,0:T(8,128)(2,1)S(1)} collective-permute-done((bf16[2,3,48,256]{3,2,1,0:T(8,128)(2,1)S(1)}, bf16[2,3,48,256]{3,2,1,0:T(8,128)(2,1)S(1)}, u32[]{:S(2)}, u32[]{:S(2)}) %collective-permute-start.27) | collective-permute-done | bytes 147488 | tf_op jit(solution)/shard_map/ppermute | solution.py:183
  129.2 15.1 %all_to_all.5.returned = bf16[8,3,48,256]{3,2,1,0:T(8,128)(2,1)S(1)} all-to-all(bf16[8,3,48,256]{3,2,1,0:T(8,128)(2,1)S(1)} %dynamic-slice_dynamic-update-slice_fusion), channel_id=1, replica_groups=mesh['section'=4,'rep'=8] {'rep'}, dimensions={0} | all-to-all | bytes 1179648 | tf_op jit(solution)/shard_map/all_to_all | solution.py:190
  (89 shorter events, 49.5 us)
Async XLA Ops:
  5.6 13.5 %collective-permute-start.2 = (bf16[3,48,1024]{2,1,0:T(8,128)(2,1)S(1)}, bf16[3,48,1024]{2,1,0:T(8,128)(2,1)S(1)}, u32[]{:S(2)}, u32[]{:S(2)}) collective-permute-start(bf16[3,48,1024]{2,1,0:T(8,128)(2,1)S(1)} %get-tuple-element.15), channel_id=1, source_target_pairs={{0,2},{1,3},{2,0},{3,1},{4,6},{5,7},{6,4},{7,5},{8,10},{9,11},{10,... | collective-permute-start | bytes 884744 | tf_op jit(solution)/shard_map/ppermute | solution.py:162
  17.4 12.8 %collective-permute-start.9 = (bf16[3,48,1024]{2,1,0:T(8,128)(2,1)S(1)}, bf16[3,48,1024]{2,1,0:T(8,128)(2,1)S(1)}, u32[]{:S(2)}, u32[]{:S(2)}) collective-permute-start(bf16[3,48,1024]{2,1,0:T(8,128)(2,1)S(1)} %get-tuple-element.20), channel_id=1, source_target_pairs={{0,1},{1,0},{2,3},{3,2},{4,5},{5,4},{6,7},{7,6},{8,9},{9,8},{10,11... | collective-permute-start | bytes 884744 | tf_op jit(solution)/shard_map/ppermute | solution.py:162
  17.4 20.1 %collective-permute-start.1 = (bf16[3,48,1024]{2,1,0:T(8,128)(2,1)S(1)}, bf16[3,48,1024]{2,1,0:T(8,128)(2,1)S(1)}, u32[]{:S(2)}, u32[]{:S(2)}) collective-permute-start(bf16[3,48,1024]{2,1,0:T(8,128)(2,1)S(1)} %get-tuple-element.14), channel_id=1, source_target_pairs={{0,4},{1,5},{2,6},{3,7},{4,0},{5,1},{6,2},{7,3},{8,12},{9,13},{10,... | collective-permute-start | bytes 884744 | tf_op jit(solution)/shard_map/ppermute | solution.py:162
  25.6 13.0 %collective-permute-start.4 = (bf16[3,48,1024]{2,1,0:T(8,128)(2,1)S(1)}, bf16[3,48,1024]{2,1,0:T(8,128)(2,1)S(1)}, u32[]{:S(2)}, u32[]{:S(2)}) collective-permute-start(bf16[3,48,1024]{2,1,0:T(8,128)(2,1)S(1)} %layer.15), channel_id=1, source_target_pairs={{0,8},{8,16},{16,24},{1,9},{9,17},{17,25},{2,10},{10,18},{18,26},{... | collective-permute-start | bytes 884744 | tf_op jit(solution)/shard_map/ppermute | solution.py:173
  30.0 14.4 %collective-permute-start.8 = (bf16[3,48,1024]{2,1,0:T(8,128)(2,1)S(1)}, bf16[3,48,1024]{2,1,0:T(8,128)(2,1)S(1)}, u32[]{:S(2)}, u32[]{:S(2)}) collective-permute-start(bf16[3,48,1024]{2,1,0:T(8,128)(2,1)S(1)} %get-tuple-element.19), channel_id=1, source_target_pairs={{0,3},{1,2},{2,1},{3,0},{4,7},{5,6},{6,5},{7,4},{8,11},{9,10},{10,... | collective-permute-start | bytes 884744 | tf_op jit(solution)/shard_map/ppermute | solution.py:162
  32.4 12.0 %collective-permute-start.10 = (bf16[3,48,1024]{2,1,0:T(8,128)(2,1)S(1)}, bf16[3,48,1024]{2,1,0:T(8,128)(2,1)S(1)}, u32[]{:S(2)}, u32[]{:S(2)}) collective-permute-start(bf16[3,48,1024]{2,1,0:T(8,128)(2,1)S(1)} %layer.18), channel_id=1, source_target_pairs={{0,8},{8,16},{16,24},{1,9},{9,17},{17,25},{2,10},{10,18},{18,26},{... | collective-permute-start | bytes 884744 | tf_op jit(solution)/shard_map/ppermute | solution.py:173
  36.0 15.1 %collective-permute-start = (bf16[3,48,1024]{2,1,0:T(8,128)(2,1)S(1)}, bf16[3,48,1024]{2,1,0:T(8,128)(2,1)S(1)}, u32[]{:S(2)}, u32[]{:S(2)}) collective-permute-start(bf16[3,48,1024]{2,1,0:T(8,128)(2,1)S(1)} %get-tuple-element.13), channel_id=1, source_target_pairs={{0,6},{1,7},{2,4},{3,5},{4,2},{5,3},{6,0},{7,1},{8,14},{9,15},{10,... | collective-permute-start | bytes 884744 | tf_op jit(solution)/shard_map/ppermute | solution.py:162
  37.5 21.0 %collective-permute-start.7 = (bf16[3,48,1024]{2,1,0:T(8,128)(2,1)S(1)}, bf16[3,48,1024]{2,1,0:T(8,128)(2,1)S(1)}, u32[]{:S(2)}, u32[]{:S(2)}) collective-permute-start(bf16[3,48,1024]{2,1,0:T(8,128)(2,1)S(1)} %get-tuple-element.18), channel_id=1, source_target_pairs={{0,5},{1,4},{2,7},{3,6},{4,1},{5,0},{6,3},{7,2},{8,13},{9,12},{10,... | collective-permute-start | bytes 884744 | tf_op jit(solution)/shard_map/ppermute | solution.py:162
  41.0 10.9 %collective-permute-start.5 = (bf16[3,48,1024]{2,1,0:T(8,128)(2,1)S(1)}, bf16[3,48,1024]{2,1,0:T(8,128)(2,1)S(1)}, u32[]{:S(2)}, u32[]{:S(2)}) collective-permute-start(bf16[3,48,1024]{2,1,0:T(8,128)(2,1)S(1)} %layer.16), channel_id=1, source_target_pairs={{0,8},{8,16},{16,24},{1,9},{9,17},{17,25},{2,10},{10,18},{18,26},{... | collective-permute-start | bytes 884744 | tf_op jit(solution)/shard_map/ppermute | solution.py:173
  46.8 11.7 %collective-permute-start.11 = (bf16[3,48,1024]{2,1,0:T(8,128)(2,1)S(1)}, bf16[3,48,1024]{2,1,0:T(8,128)(2,1)S(1)}, u32[]{:S(2)}, u32[]{:S(2)}) collective-permute-start(bf16[3,48,1024]{2,1,0:T(8,128)(2,1)S(1)} %layer.19), channel_id=1, source_target_pairs={{0,8},{8,16},{16,24},{1,9},{9,17},{17,25},{2,10},{10,18},{18,26},{... | collective-permute-start | bytes 884744 | tf_op jit(solution)/shard_map/ppermute | solution.py:173
  49.7 20.9 %collective-permute-start.6 = (bf16[3,48,1024]{2,1,0:T(8,128)(2,1)S(1)}, bf16[3,48,1024]{2,1,0:T(8,128)(2,1)S(1)}, u32[]{:S(2)}, u32[]{:S(2)}) collective-permute-start(bf16[3,48,1024]{2,1,0:T(8,128)(2,1)S(1)} %get-tuple-element.17), channel_id=1, source_target_pairs={{0,7},{1,6},{2,5},{3,4},{4,3},{5,2},{6,1},{7,0},{8,15},{9,14},{10,... | collective-permute-start | bytes 884744 | tf_op jit(solution)/shard_map/ppermute | solution.py:162
  54.1 9.7 %collective-permute-start.13 = (bf16[3,48,1024]{2,1,0:T(8,128)(2,1)S(1)}, bf16[3,48,1024]{2,1,0:T(8,128)(2,1)S(1)}, u32[]{:S(2)}, u32[]{:S(2)}) collective-permute-start(bf16[3,48,1024]{2,1,0:T(8,128)(2,1)S(1)} %layer.17), channel_id=1, source_target_pairs={{0,8},{8,16},{16,24},{1,9},{9,17},{17,25},{2,10},{10,18},{18,26},{... | collective-permute-start | bytes 884744 | tf_op jit(solution)/shard_map/ppermute | solution.py:173
  60.9 10.3 %collective-permute-start.12 = (bf16[3,48,1024]{2,1,0:T(8,128)(2,1)S(1)}, bf16[3,48,1024]{2,1,0:T(8,128)(2,1)S(1)}, u32[]{:S(2)}, u32[]{:S(2)}) collective-permute-start(bf16[3,48,1024]{2,1,0:T(8,128)(2,1)S(1)} %layer.20), channel_id=1, source_target_pairs={{0,8},{8,16},{16,24},{1,9},{9,17},{17,25},{2,10},{10,18},{18,26},{... | collective-permute-start | bytes 884744 | tf_op jit(solution)/shard_map/ppermute | solution.py:173
  66.2 11.8 %collective-permute-start.18 = (bf16[3,48,1024]{2,1,0:T(8,128)(2,1)S(1)}, bf16[3,48,1024]{2,1,0:T(8,128)(2,1)S(1)}, u32[]{:S(2)}, u32[]{:S(2)}) collective-permute-start(bf16[3,48,1024]{2,1,0:T(8,128)(2,1)S(1)} %layer.22), channel_id=1, source_target_pairs={{0,8},{8,16},{16,24},{1,9},{9,17},{17,25},{2,10},{10,18},{18,26},{... | collective-permute-start | bytes 884744 | tf_op jit(solution)/shard_map/ppermute | solution.py:173
  73.5 10.1 %collective-permute-start.14 = (bf16[3,48,1024]{2,1,0:T(8,128)(2,1)S(1)}, bf16[3,48,1024]{2,1,0:T(8,128)(2,1)S(1)}, u32[]{:S(2)}, u32[]{:S(2)}) collective-permute-start(bf16[3,48,1024]{2,1,0:T(8,128)(2,1)S(1)} %layer.21), channel_id=1, source_target_pairs={{0,8},{8,16},{16,24},{1,9},{9,17},{17,25},{2,10},{10,18},{18,26},{... | collective-permute-start | bytes 884744 | tf_op jit(solution)/shard_map/ppermute | solution.py:173
  80.3 24.3 %collective-permute-start.23 = (bf16[3,48,1024]{2,1,0:T(8,128)(2,1)S(1)}, bf16[3,48,1024]{2,1,0:T(8,128)(2,1)S(1)}, u32[]{:S(2)}, u32[]{:S(2)}) collective-permute-start(bf16[3,48,1024]{2,1,0:T(8,128)(2,1)S(1)} %layer.24), channel_id=1, source_target_pairs={{0,8},{8,16},{16,24},{1,9},{9,17},{17,25},{2,10},{10,18},{18,26},{... | collective-permute-start | bytes 884744 | tf_op jit(solution)/shard_map/ppermute | solution.py:173
  90.6 16.9 %collective-permute-start.15 = (bf16[4,3,48,256]{3,2,1,0:T(8,128)(2,1)S(1)}, bf16[4,3,48,256]{3,2,1,0:T(8,128)(2,1)}, u32[]{:S(2)}, u32[]{:S(2)}) collective-permute-start(bf16[4,3,48,256]{3,2,1,0:T(8,128)(2,1)S(1)} %get-tuple-element.23), channel_id=1, source_target_pairs={{24,16},{25,17},{26,18},{27,19},{28,20},{29,21},{30,22},{31,23}} | collective-permute-start | bytes 884744 | tf_op jit(solution)/shard_map/ppermute | solution.py:183
  92.0 16.2 %collective-permute-start.16 = (bf16[4,3,48,256]{3,2,1,0:T(8,128)(2,1)S(1)}, bf16[4,3,48,256]{3,2,1,0:T(8,128)(2,1)}, u32[]{:S(2)}, u32[]{:S(2)}) collective-permute-start(bf16[4,3,48,256]{3,2,1,0:T(8,128)(2,1)S(1)} %get-tuple-element.22), channel_id=1, source_target_pairs={{24,8},{25,9},{26,10},{27,11},{28,12},{29,13},{30,14},{31,15}} | collective-permute-start | bytes 884744 | tf_op jit(solution)/shard_map/ppermute | solution.py:183
  93.4 19.7 %collective-permute-start.17 = (bf16[4,3,48,256]{3,2,1,0:T(8,128)(2,1)S(1)}, bf16[4,3,48,256]{3,2,1,0:T(8,128)(2,1)}, u32[]{:S(2)}, u32[]{:S(2)}) collective-permute-start(bf16[4,3,48,256]{3,2,1,0:T(8,128)(2,1)S(1)} %get-tuple-element.21), channel_id=1, source_target_pairs={{24,0},{25,1},{26,2},{27,3},{28,4},{29,5},{30,6},{31,7}} | collective-permute-start | bytes 884744 | tf_op jit(solution)/shard_map/ppermute | solution.py:183
  100.1 14.1 %collective-permute-start.24 = (bf16[3,48,1024]{2,1,0:T(8,128)(2,1)S(1)}, bf16[3,48,1024]{2,1,0:T(8,128)(2,1)S(1)}, u32[]{:S(2)}, u32[]{:S(2)}) collective-permute-start(bf16[3,48,1024]{2,1,0:T(8,128)(2,1)S(1)} %layer.25), channel_id=1, source_target_pairs={{0,8},{8,16},{16,24},{1,9},{9,17},{17,25},{2,10},{10,18},{18,26},{... | collective-permute-start | bytes 884744 | tf_op jit(solution)/shard_map/ppermute | solution.py:173
  104.6 13.3 %collective-permute-start.20 = (bf16[2,3,48,256]{3,2,1,0:T(8,128)(2,1)S(1)}, bf16[2,3,48,256]{3,2,1,0:T(8,128)(2,1)S(1)}, u32[]{:S(2)}, u32[]{:S(2)}) collective-permute-start(bf16[2,3,48,256]{3,2,1,0:T(8,128)(2,1)S(1)} %get-tuple-element.25), channel_id=1, source_target_pairs={{24,16},{25,17},{26,18},{27,19},{28,20},{29,21},{30,22},{31,23}} | collective-permute-start | bytes 442376 | tf_op jit(solution)/shard_map/ppermute | solution.py:183
  107.6 11.6 %collective-permute-start.21 = (bf16[2,3,48,256]{3,2,1,0:T(8,128)(2,1)S(1)}, bf16[2,3,48,256]{3,2,1,0:T(8,128)(2,1)S(1)}, u32[]{:S(2)}, u32[]{:S(2)}) collective-permute-start(bf16[2,3,48,256]{3,2,1,0:T(8,128)(2,1)S(1)} %get-tuple-element.26), channel_id=1, source_target_pairs={{24,8},{25,9},{26,10},{27,11},{28,12},{29,13},{30,14},{31,15}} | collective-permute-start | bytes 442376 | tf_op jit(solution)/shard_map/ppermute | solution.py:183
  108.2 14.2 %collective-permute-start.22 = (bf16[2,3,48,256]{3,2,1,0:T(8,128)(2,1)S(1)}, bf16[2,3,48,256]{3,2,1,0:T(8,128)(2,1)S(1)}, u32[]{:S(2)}, u32[]{:S(2)}) collective-permute-start(bf16[2,3,48,256]{3,2,1,0:T(8,128)(2,1)S(1)} %get-tuple-element.24), channel_id=1, source_target_pairs={{24,0},{25,1},{26,2},{27,3},{28,4},{29,5},{30,6},{31,7}} | collective-permute-start | bytes 442376 | tf_op jit(solution)/shard_map/ppermute | solution.py:183
  117.9 11.0 %collective-permute-start.27 = (bf16[2,3,48,256]{3,2,1,0:T(8,128)(2,1)S(1)}, bf16[2,3,48,256]{3,2,1,0:T(8,128)(2,1)S(1)}, u32[]{:S(2)}, u32[]{:S(2)}) collective-permute-start(bf16[2,3,48,256]{3,2,1,0:T(8,128)(2,1)S(1)} %get-tuple-element.27), channel_id=1, source_target_pairs={{24,0},{25,1},{26,2},{27,3},{28,4},{29,5},{30,6},{31,7}} | collective-permute-start | bytes 442376 | tf_op jit(solution)/shard_map/ppermute | solution.py:183
  (14 other events, 91.0 us)

commit v2 on v1

v2 whole, which is shorter than its diff:
```python
import functools
import jax
import jax.numpy as jnp
from jax import lax
from jax.experimental import pallas as pl
from jax.experimental.pallas import tpu as pltpu
from jax.sharding import PartitionSpec as P

epsilon = 1e-05
STREAMS = 2
SMALL_VMEM = 12 * 1024 * 1024
VMEM_LIMIT = 24 * 1024 * 1024

ANY = pl.BlockSpec(memory_space=pl.ANY)
SMEM = pl.BlockSpec(memory_space=pltpu.SMEM)
VMEM = pl.BlockSpec(memory_space=pltpu.VMEM)


def upright(row):
    return jnp.transpose(jnp.broadcast_to(row, (row.shape[1], row.shape[1])))


def open_kernel(out):
    out[...] = jnp.zeros_like(out)


def dispatch_kernel(sizes, placement, widths, ids, tokens, gains, opened, target, table, *chunks):
    batches, row_count, slot_count, capacity, depth = sizes
    me = lax.axis_index("rep")
    slot_rows = batches * capacity
    replica_count = placement.shape[0]
    starts, slots = [], []
    for replica in range(replica_count):
        slot = placement[replica]
        holder = lax.div(slot, slot_count)
        starts.append(((holder ^ me) * slot_count + slot - holder * slot_count) * slot_rows)
        slots.append(slot)
    features = lax.broadcasted_iota(jnp.int32, (1, depth), 1)
    for j in range(slot_count):
        width = jnp.int32(0)
        for replica in range(replica_count):
            width = width + jnp.where(slots[replica] == me * slot_count + j, widths[replica], 0)
        inverse = 1.0 / jnp.maximum(jnp.full((1, depth), width), 1).astype(jnp.float32)
        table[j, 0:1] = gains[j]
        table[j, 1:2] = jnp.where(features < width, inverse, 0.0)

    square = (row_count, row_count)
    early = lax.broadcasted_iota(jnp.int32, square, 0) < lax.broadcasted_iota(jnp.int32, square, 1)
    rows = []
    for m in range(batches):
        own = ids[m]
        same = jnp.where((upright(own) == own) & early, 1, 0)
        row = jnp.sum(same, axis=0, keepdims=True) + m * capacity
        for replica, start in enumerate(starts):
            row = row + jnp.where(own == replica, start, 0)
        target[m] = row
        rows.append(row)
    row = jnp.concatenate(rows, axis=1)
    chunk_rows = slot_count * slot_rows
    source = jnp.concatenate([tokens[m] for m in range(batches)], axis=0)
    for i, chunk in enumerate(chunks):
        wanted = lax.broadcasted_iota(jnp.int32, (chunk_rows, batches * row_count), 0)
        picked = jnp.where(row == wanted + i * chunk_rows, 1.0, 0.0).astype(jnp.bfloat16)
        moved = jnp.dot(picked, source, preferred_element_type=jnp.float32).astype(jnp.bfloat16)
        for j in range(slot_count):
            chunk[j] = moved[j * slot_rows : (j + 1) * slot_rows]


def route_kernel(target, token, picked):
    for m in range(picked.shape[0]):
        wanted = upright(target[m])[:, :1]
        place = lax.broadcasted_iota(jnp.int32, picked.shape[1:], 1)
        picked[m] = jnp.where(wanted == place, 1.0, 0.0).astype(jnp.bfloat16)


def layer_kernel(has_first, has_arrived, before_count, forwards, parts, *refs):
    refs = list(refs)
    first = refs.pop(0) if has_first else None
    arrived = refs.pop(0) if has_arrived else None
    before = [refs.pop(0) for _ in range(before_count)]
    table, weight, _ = refs[:3]
    outs = refs[3:]
    if first is not None and arrived is not None:
        rows = jnp.where(lax.axis_index("section") == 0, first[0], arrived[0])
    else:
        rows = first[0] if arrived is None else arrived[0]
    rows = rows.astype(jnp.float32)
    gain, inverse = table[0, 0:1], table[0, 1:2]
    rows = jnp.where(inverse > 0.0, rows, 0.0)
    mean_square = jnp.sum(rows * rows * inverse, axis=1, keepdims=True)
    lowered = (rows * lax.rsqrt(mean_square + epsilon) * gain).astype(jnp.bfloat16)
    projected = jnp.dot(lowered, weight[0], preferred_element_type=jnp.float32)
    gate = projected * jax.nn.sigmoid(projected)
    done = (rows + jnp.where(inverse > 0.0, gate, 0.0)).astype(jnp.bfloat16)
    if forwards:
        outs.pop(0)[0] = done
    for s in range(parts):
        size = done.shape[1] // parts
        for at, ref in enumerate(before):
            outs[s][at, 0] = ref[0, :, s * size : (s + 1) * size]
        outs[s][before_count, 0] = done[:, s * size : (s + 1) * size]


def layer(first, arrived, before, token, table, weight, forwards, parts, held):
    given = [a for a in (first, arrived) if a is not None] + before
    slot_count, slot_rows, depth = given[0].shape
    block = pl.BlockSpec((1, slot_rows, depth), lambda j: (j, 0, 0))
    out_specs, out_shape = [], []
    if forwards:
        out_specs.append(block)
        out_shape.append(jax.ShapeDtypeStruct(given[0].shape, jnp.bfloat16))
    for _ in range(parts):
        size = depth // parts
        out_specs.append(pl.BlockSpec((held, 1, slot_rows, size), lambda j: (0, j, 0, 0)))
        out_shape.append(
            jax.ShapeDtypeStruct((held, slot_count, slot_rows, size), jnp.bfloat16)
        )
    return pl.pallas_call(
        functools.partial(
            layer_kernel, first is not None, arrived is not None, len(before), forwards, parts
        ),
        grid=(slot_count,),
        in_specs=[block] * len(given)
        + [
            pl.BlockSpec((1, 2, depth), lambda j: (j, 0, 0)),
            pl.BlockSpec((1, depth, depth), lambda j: (j, 0, 0)),
            ANY,
        ],
        out_specs=out_specs,
        out_shape=out_shape,
        compiler_params=pltpu.CompilerParams(vmem_limit_bytes=SMALL_VMEM),
        cost_estimate=pl.CostEstimate(
            flops=2 * slot_count * slot_rows * depth * depth,
            bytes_accessed=2 * slot_count * depth * (depth + 3 * slot_rows),
            transcendentals=0,
        ),
        name="layer",
    )(*given, table, weight, token)


def chosen(candidates):
    section = lax.axis_index("section")
    value = candidates[0]
    for s in range(1, len(candidates)):
        value = jnp.where(section == s, candidates[s], value)
    return value


def pick_kernel(sections, groups, token, *refs):
    outs = list(refs[sections * len(groups) :])
    for g, group in enumerate(groups):
        mine = refs[g * sections : (g + 1) * sections]
        for h in range(len(group)):
            out = outs.pop(0)
            for j in range(out.shape[0]):
                out[j] = chosen([ref[h, j] for ref in mine])


def combine_kernel(sections, direct, spans, picked, acc, *refs):
    out, refs = refs[-1], refs[:-1]
    rows = []
    for at in range(len(spans)):
        mine = refs[at * sections : (at + 1) * sections] if direct else refs[at : at + 1]
        for j in range(mine[0].shape[1] if direct else mine[0].shape[0]):
            rows.append(chosen([ref[0, j] for ref in mine]) if direct else mine[0][j])
    flat = jnp.concatenate(rows, axis=0)
    for m in range(out.shape[0]):
        select = jnp.concatenate([picked[m, :, low:high] for low, high in spans], axis=1)
        value = jnp.dot(select, flat, preferred_element_type=jnp.float32)
        if acc is not None:
            value = value + acc[m]
        out[m] = value.astype(out.dtype)


def schedule(rep_count):
    order = [0, 1, 4, 3, 5] + list(range(6, rep_count)) + [2]
    early = order[:-2]
    size = max(3, -(-len(early) // 4))
    groups = [early[at : at + size] for at in range(0, len(early), size)]
    return order, groups, order[-2:]


def on_device(tokens, replica_of_row, widths, placement, gains, weights):
    batches, row_count, depth = tokens.shape
    rep_count = lax.axis_size("rep")
    section_count = lax.axis_size("section")
    slot_count = weights.shape[1]
    replica_count = widths.shape[0]
    capacity = (3 * row_count + 2 * replica_count - 1) // (2 * replica_count)
    last = section_count - 1
    part = depth // section_count
    slot_rows = batches * capacity
    chunk_rows = slot_count * slot_rows

    gain = gains.reshape(slot_count, 1, depth)
    weight = weights.reshape(slot_count, depth, depth)
    ids = replica_of_row.reshape(batches, 1, row_count)
    chunk_shape = jax.ShapeDtypeStruct((slot_count, slot_rows, depth), jnp.bfloat16)
    opened = pl.pallas_call(
        open_kernel,
        in_specs=[],
        out_specs=VMEM,
        out_shape=jax.ShapeDtypeStruct((8, 128), jnp.float32),
        compiler_params=pltpu.CompilerParams(vmem_limit_bytes=1024 * 1024),
        cost_estimate=pl.CostEstimate(
            flops=16 * 1024**3, bytes_accessed=64 * 1024**2, transcendentals=0
        ),
        name="open",
    )()
    target, table, *outgoing = pl.pallas_call(
        functools.partial(
            dispatch_kernel, (batches, row_count, slot_count, capacity, depth)
        ),
        in_specs=[SMEM, SMEM, VMEM, VMEM, VMEM, ANY],
        out_specs=[VMEM] * (rep_count + 2),
        out_shape=[
            jax.ShapeDtypeStruct(ids.shape, jnp.int32),
            jax.ShapeDtypeStruct((slot_count, 2, depth), jnp.float32),
        ]
        + [chunk_shape] * rep_count,
        compiler_params=pltpu.CompilerParams(vmem_limit_bytes=VMEM_LIMIT),
        cost_estimate=pl.CostEstimate(
            flops=2 * batches * row_count * rep_count * chunk_rows * depth,
            bytes_accessed=2 * depth * (batches * row_count + rep_count * chunk_rows),
            transcendentals=0,
        ),
        name="dispatch",
    )(placement, widths, ids, tokens, gain, opened)

    def traded(x, i):
        if i == 0:
            return x
        return lax.ppermute(x, "rep", [(d, d ^ i) for d in range(rep_count)])

    order, groups, direct = schedule(rep_count)

    def arriving(x, i):
        if i == 0:
            return x
        return lax.ppermute(x, ("section", "rep"), [(d, d ^ i) for d in range(rep_count)])

    entering = {i: arriving(outgoing[i], i) for i in order}

    def sent_back(pieces, hop):
        sent = []
        for s, piece in enumerate(pieces):
            if s != last or hop != 0:
                hops = [(last * rep_count + d, s * rep_count + (d ^ hop)) for d in range(rep_count)]
                piece = lax.ppermute(piece, ("section", "rep"), hops)
            sent.append(piece)
        return sent

    lag = STREAMS * last
    inbound, finished, back = {}, {}, {}
    token = target
    picked = None
    for n in range(rep_count + lag):
        first = entering[order[n]] if n < rep_count else None
        arrived = inbound.get(n)
        closing = groups + [[i] for i in direct]
        group = next((g for g in closing if n >= lag and g[-1] == order[n - lag]), None)
        before = [finished[i] for i in group[:-1]] if group else []
        opens = n >= lag and group is None
        forward = [(s, s + 1) for s in range(last) if 0 <= n - STREAMS * s < rep_count]
        forwards = n < rep_count + lag - STREAMS or opens
        made = layer(
            first,
            arrived,
            before,
            token,
            table,
            weight,
            forwards,
            section_count if group else 0,
            len(group) if group else 0,
        )
        token = made[0]
        if n < rep_count + lag - STREAMS:
            inbound[n + STREAMS] = lax.ppermute(made[0], "section", forward)
        if opens:
            finished[order[n - lag]] = made[0]
        if group:
            hop = group[0] if group[0] in direct else 0
            back[group[0]] = sent_back(made[-section_count:], hop)
        if n == 1:
            token = picked = pl.pallas_call(
                route_kernel,
                in_specs=[VMEM, ANY],
                out_specs=VMEM,
                out_shape=jax.ShapeDtypeStruct(
                    (batches, row_count, rep_count * chunk_rows), jnp.bfloat16
                ),
                compiler_params=pltpu.CompilerParams(vmem_limit_bytes=SMALL_VMEM),
                name="route",
            )(target, token)

    mine = pl.pallas_call(
        functools.partial(pick_kernel, section_count, groups),
        in_specs=[ANY] + [VMEM] * (section_count * len(groups)),
        out_specs=[VMEM] * (rep_count - len(direct)),
        out_shape=[jax.ShapeDtypeStruct((slot_count, slot_rows, part), jnp.bfloat16)]
        * (rep_count - len(direct)),
        compiler_params=pltpu.CompilerParams(vmem_limit_bytes=SMALL_VMEM),
        name="pick",
    )(token, *[piece for group in groups for piece in back[group[0]]])
    early = order[: len(mine)]
    returned = [traded(piece, i) for i, piece in zip(early, mine)]

    def combined(these, acc, given, dtype, is_direct):
        spans = [(i * chunk_rows, (i + 1) * chunk_rows) for i in these]

        def kernel(picked, *refs):
            refs = list(refs)
            some = refs.pop(0) if acc is not None else None
            combine_kernel(section_count, is_direct, spans, picked, some, *refs)

        extra = [] if acc is None else [acc]
        return pl.pallas_call(
            kernel,
            in_specs=[VMEM] * (1 + len(extra) + len(given)),
            out_specs=VMEM,
            out_shape=jax.ShapeDtypeStruct((batches, row_count, part), dtype),
            compiler_params=pltpu.CompilerParams(vmem_limit_bytes=SMALL_VMEM),
            name="combine",
        )(picked, *extra, *given)

    acc = combined(early, None, returned, jnp.float32, False)
    late = [piece for i in direct for piece in back[i]]
    return combined(direct, acc, late, jnp.bfloat16, True)


def solution(mesh):
    placed = (
        P(None, "rep", None),
        P(None, "rep", None),
        P(),
        P(),
        P("section", "rep", None),
        P("section", "rep", None, None),
    )

    return jax.shard_map(
        on_device, mesh=mesh, in_specs=placed, out_specs=P(None, "rep", "section"), check_vma=False
    )
```

time: 147 us -> 124 us (0.84)
  blocking collectives: 15.1 us -> 0 us
  waiting for transfers between devices: 19.1 us -> 28.6 us
  local copies, waits for them, and re-layouts: 9.19 us -> 1.24 us
  Pallas kernels: 36.6 us -> 28.8 us
  other arithmetic: 1.73 us -> 0 us
    all_to_all x1 -> x0, blocking collectives: 15.1 us -> none  [on_device(): lax.all_to_all(by_owner, 'rep', split_axis=0, concat_axis=0, tiled=True)]
    ppermute x21 -> x33, waiting for transfers between devices: 19.1 us -> 27.4 us  [the longest x14 22.9 us: sent_back(): piece = lax.ppermute(piece, ('section', 'rep'), hops)]
    unnamed x28 -> x12, local copies, waits for them, and re-layouts: 9.1 us -> 1.24 us
    pallas_call x16 -> x20, Pallas kernels: 36.6 us -> 28.8 us  [the longest x14 24.6 us: layer(): pl.pallas_call(functools.partial(layer_kernel, first is not None, arrived...]
    ppermute x21 -> x33, starting transfers between devices: 55.4 us -> 54.6 us  [the longest x12 22.7 us: on_device(): inbound[n + STREAMS] = lax.ppermute(made[0], 'section', forward)]
    ppermute x7 -> x5, starting transfers between devices: 8.76 us -> 9.44 us  [traded(): return lax.ppermute(x, 'rep', [(d, d ^ i) for d in range(rep_count)])]
  transfers between devices with their start and end apart: 28 -> 38, of which waited for: 7 -> 8; matrix products, arithmetic and copies ran while one was open for 1% -> 0% of each run, Pallas kernels for 22% -> 21%
where the time goes in v2:
time: 124 us; the launch traced here: 123 us
  starting transfers between devices  64 us (52%)
  Pallas kernels  28.8 us (23%)
  waiting for transfers between devices  28.6 us (23%)
  local copies, waits for them, and re-layouts  1.24 us (1%)
    pallas_call x14, Pallas kernels, layer(): pl.pallas_call(functools.partial(layer_kernel, first is not None, arrived...  24.6 us
    ppermute x14, waiting for transfers between devices, sent_back(): piece = lax.ppermute(piece, ('section', 'rep'), hops)  22.9 us
    ppermute x12, starting transfers between devices, on_device(): inbound[n + STREAMS] = lax.ppermute(made[0], 'section', forward)  22.7 us
    ppermute x7, starting transfers between devices, arriving(): lax.ppermute(x, ('section', 'rep'), [(d, d ^ i) for d in range(rep_count)])  20.1 us
    ppermute x14, starting transfers between devices, sent_back(): piece = lax.ppermute(piece, ('section', 'rep'), hops)  11.8 us
    ppermute x5, starting transfers between devices, traded(): return lax.ppermute(x, 'rep', [(d, d ^ i) for d in range(rep_count)])  9.44 us
    ppermute x12, waiting for transfers between devices, on_device(): inbound[n + STREAMS] = lax.ppermute(made[0], 'section', forward)  4.47 us
  transfers between devices with their start and end apart: 38, of which 8 were waited for; matrix products, arithmetic and copies ran while one was open for 0% of the time, Pallas kernels for 21%

profile of v2, /device:TPU:0, one launch (start us, length us, event | category | flops | bytes accessed | tf_op | source)
XLA Modules:
  0.0 123.3 jit_solution(14339665536378573563)
XLA Ops:
  1.3 2.1 %dispatch.1 = (s32[4,1,128]{2,1,0:T(1,128)S(1)}, f32[3,2,1024]{2,1,0:T(2,128)S(1)}, bf16[3,48,1024]{2,1,0:T(8,128)(2,1)S(1)}, bf16[3,48,1024]{2,1,0:T(8,128)(2,1...) custom-call(s32[16]{0:T(128)S(1)} %copy-done.4, ...), custom_call_target="tpu_custom_call" | custom-call | flops 1207959552 | bytes 3407872 | tf_op jit(solution)/shard_map/dispatch/pallas_call | solution.py:210
  3.4 2.4 %collective-permute-start = (bf16[3,48,1024]{2,1,0:T(8,128)(2,1)S(1)}, bf16[3,48,1024]{2,1,0:T(8,128)(2,1)S(1)}, u32[]{:S(2)}, u32[]{:S(2)}) collective-permute-start(bf16[3,48,1024]{2,1,0:T(8,128)(2,1)S(1)} %get-tuple-element.40), channel_id=1, source_target_pairs={{0,1},{1,0},{2,3},{3,2},{4,5},{5,4},{6,7},{7,6}} | collective-permute-start | bytes 884744 | tf_op jit(solution)/shard_map/ppermute | solution.py:240
  5.8 1.7 %layer.14.refs_3_ = bf16[3,48,1024]{2,1,0:T(8,128)(2,1)S(1)} custom-call(bf16[3,48,1024]{2,1,0:T(8,128)(2,1)S(1)} %get-tuple-element.42.refs_0_, f32[3,2,1024]{2,1,0:T(2,128)S(1)} %get-tuple-element.41.refs_1_.refs_2_.refs_3_, bf16[3,1024,1024]{2,1,0:T(8,128)(2,1)S(1)} %bitcast.3, s32[4,1,128]{2,1,0:T(1,128)S(1)} %get-tuple-element.39.refs_3_.target), custom_call_target="tpu_custom_call" | custom-call | flops 301989888 | bytes 7176192 | tf_op jit(solution)/shard_map/layer/pallas_call | solution.py:118
  7.6 3.2 %collective-permute-start.6 = (bf16[3,48,1024]{2,1,0:T(8,128)(2,1)S(1)}, bf16[3,48,1024]{2,1,0:T(8,128)(2,1)S(1)}, u32[]{:S(2)}, u32[]{:S(2)}) collective-permute-start(bf16[3,48,1024]{2,1,0:T(8,128)(2,1)S(1)} %layer.14.refs_3_), channel_id=1, source_target_pairs={{0,8},{1,9},{2,10},{3,11},{4,12},{5,13},{6,14},{7,15}} | collective-permute-start | bytes 884744 | tf_op jit(solution)/shard_map/ppermute | solution.py:279
  10.8 3.4 %collective-permute-start.5 = (bf16[3,48,1024]{2,1,0:T(8,128)(2,1)S(1)}, bf16[3,48,1024]{2,1,0:T(8,128)(2,1)S(1)}, u32[]{:S(2)}, u32[]{:S(2)}) collective-permute-start(bf16[3,48,1024]{2,1,0:T(8,128)(2,1)S(1)} %get-tuple-element.46), channel_id=1, source_target_pairs={{0,4},{1,5},{2,6},{3,7},{4,0},{5,1},{6,2},{7,3}} | collective-permute-start | bytes 884744 | tf_op jit(solution)/shard_map/ppermute | solution.py:240
  14.3 2.3 %collective-permute-start.3 = (bf16[3,48,1024]{2,1,0:T(8,128)(2,1)S(1)}, bf16[3,48,1024]{2,1,0:T(8,128)(2,1)S(1)}, u32[]{:S(2)}, u32[]{:S(2)}) collective-permute-start(bf16[3,48,1024]{2,1,0:T(8,128)(2,1)S(1)} %get-tuple-element.45), channel_id=1, source_target_pairs={{0,3},{1,2},{2,1},{3,0},{4,7},{5,6},{6,5},{7,4}} | collective-permute-start | bytes 884744 | tf_op jit(solution)/shard_map/ppermute | solution.py:240
  19.6 3.3 %collective-permute-start.8 = (bf16[3,48,1024]{2,1,0:T(8,128)(2,1)S(1)}, bf16[3,48,1024]{2,1,0:T(8,128)(2,1)S(1)}, u32[]{:S(2)}, u32[]{:S(2)}) collective-permute-start(bf16[3,48,1024]{2,1,0:T(8,128)(2,1)S(1)} %get-tuple-element.47), channel_id=1, source_target_pairs={{0,5},{1,4},{2,7},{3,6},{4,1},{5,0},{6,3},{7,2}} | collective-permute-start | bytes 884744 | tf_op jit(solution)/shard_map/ppermute | solution.py:240
  23.3 1.8 %layer.16.refs_4_ = bf16[3,48,1024]{2,1,0:T(8,128)(2,1)S(1)} custom-call(bf16[3,48,1024]{2,1,0:T(8,128)(2,1)S(1)} %collective-permute-done.5.refs_0_, bf16[3,48,1024]{2,1,0:T(8,128)(2,1)S(1)} %collective-permute-done.6.refs_1_, f32[3,2,1024]{2,1,0:T(2,128)S(1)} %get-tuple-element.41.refs_1_.refs_2_.refs_3_, bf16[3,1024,1024]{2,1,0:T(8,128)(2,1)S(1)} %bitcast.5, ...), custom_call_target="tpu_custom_call" | custom-call | flops 301989888 | bytes 7176192 | tf_op jit(solution)/shard_map/layer/pallas_call | solution.py:118
  26.3 3.4 %collective-permute-start.2 = (bf16[3,48,1024]{2,1,0:T(8,128)(2,1)S(1)}, bf16[3,48,1024]{2,1,0:T(8,128)(2,1)S(1)}, u32[]{:S(2)}, u32[]{:S(2)}) collective-permute-start(bf16[3,48,1024]{2,1,0:T(8,128)(2,1)S(1)} %get-tuple-element.44), channel_id=1, source_target_pairs={{0,6},{1,7},{2,4},{3,5},{4,2},{5,3},{6,0},{7,1}} | collective-permute-start | bytes 884744 | tf_op jit(solution)/shard_map/ppermute | solution.py:240
  29.8 1.8 %layer.17.refs_4_ = bf16[3,48,1024]{2,1,0:T(8,128)(2,1)S(1)} custom-call(bf16[3,48,1024]{2,1,0:T(8,128)(2,1)S(1)} %collective-permute-done.3.refs_0_, bf16[3,48,1024]{2,1,0:T(8,128)(2,1)S(1)} %collective-permute-done.4.refs_1_, f32[3,2,1024]{2,1,0:T(2,128)S(1)} %get-tuple-element.41.refs_1_.refs_2_.refs_3_, bf16[3,1024,1024]{2,1,0:T(8,128)(2,1)S(1)} %bitcast.6, ...), custom_call_target="tpu_custom_call" | custom-call | flops 301989888 | bytes 7176192 | tf_op jit(solution)/shard_map/layer/pallas_call | solution.py:118
  32.9 2.6 %collective-permute-start.11 = (bf16[3,48,1024]{2,1,0:T(8,128)(2,1)S(1)}, bf16[3,48,1024]{2,1,0:T(8,128)(2,1)S(1)}, u32[]{:S(2)}, u32[]{:S(2)}) collective-permute-start(bf16[3,48,1024]{2,1,0:T(8,128)(2,1)S(1)} %get-tuple-element.48), channel_id=1, source_target_pairs={{0,7},{1,6},{2,5},{3,4},{4,3},{5,2},{6,1},{7,0}} | collective-permute-start | bytes 884744 | tf_op jit(solution)/shard_map/ppermute | solution.py:240
  35.5 1.8 %layer.18.refs_4_ = bf16[3,48,1024]{2,1,0:T(8,128)(2,1)S(1)} custom-call(bf16[3,48,1024]{2,1,0:T(8,128)(2,1)S(1)} %collective-permute-done.8.refs_0_, bf16[3,48,1024]{2,1,0:T(8,128)(2,1)S(1)} %collective-permute-done.9.refs_1_, f32[3,2,1024]{2,1,0:T(2,128)S(1)} %get-tuple-element.41.refs_1_.refs_2_.refs_3_, bf16[3,1024,1024]{2,1,0:T(8,128)(2,1)S(1)} %bitcast.7, ...), custom_call_target="tpu_custom_call" | custom-call | flops 301989888 | bytes 7176192 | tf_op jit(solution)/shard_map/layer/pallas_call | solution.py:118
  37.2 2.5 %collective-permute-start.12 = (bf16[3,48,1024]{2,1,0:T(8,128)(2,1)S(1)}, bf16[3,48,1024]{2,1,0:T(8,128)(2,1)S(1)}, u32[]{:S(2)}, u32[]{:S(2)}) collective-permute-start(bf16[3,48,1024]{2,1,0:T(8,128)(2,1)S(1)} %layer.18.refs_4_), channel_id=1, source_target_pairs={{0,8},{8,16},{16,24},{1,9},{9,17},{17,25},{2,10},{10,18},{18,26},{... | collective-permute-start | bytes 884744 | tf_op jit(solution)/shard_map/ppermute | solution.py:279
  39.7 2.8 %collective-permute-start.1 = (bf16[3,48,1024]{2,1,0:T(8,128)(2,1)S(1)}, bf16[3,48,1024]{2,1,0:T(8,128)(2,1)S(1)}, u32[]{:S(2)}, u32[]{:S(2)}) collective-permute-start(bf16[3,48,1024]{2,1,0:T(8,128)(2,1)S(1)} %get-tuple-element.43), channel_id=1, source_target_pairs={{0,2},{1,3},{2,0},{3,1},{4,6},{5,7},{6,4},{7,5}} | collective-permute-start | bytes 884744 | tf_op jit(solution)/shard_map/ppermute | solution.py:240
  42.5 1.8 %layer.19.refs_4_ = bf16[3,48,1024]{2,1,0:T(8,128)(2,1)S(1)} custom-call(bf16[3,48,1024]{2,1,0:T(8,128)(2,1)S(1)} %collective-permute-done.2.refs_0_, bf16[3,48,1024]{2,1,0:T(8,128)(2,1)S(1)} %collective-permute-done.7.refs_1_, f32[3,2,1024]{2,1,0:T(2,128)S(1)} %get-tuple-element.41.refs_1_.refs_2_.refs_3_, bf16[3,1024,1024]{2,1,0:T(8,128)(2,1)S(1)} %bitcast.8, ...), custom_call_target="tpu_custom_call" | custom-call | flops 301989888 | bytes 7176192 | tf_op jit(solution)/shard_map/layer/pallas_call | solution.py:118
  48.5 4.4 %collective-permute-start.14 = (bf16[3,48,1024]{2,1,0:T(8,128)(2,1)S(1)}, bf16[3,48,1024]{2,1,0:T(8,128)(2,1)S(1)}, u32[]{:S(2)}, u32[]{:S(2)}) collective-permute-start(bf16[3,48,1024]{2,1,0:T(8,128)(2,1)S(1)} %layer.20.refs_4_.refs_1_), channel_id=1, source_target_pairs={{0,8},{8,16},{16,24},{1,9},{9,17},{17,25},{2,10},{10,18},{18,26},{... | collective-permute-start | bytes 884744 | tf_op jit(solution)/shard_map/ppermute | solution.py:279
  54.9 4.4 %collective-permute-start.13 = (bf16[3,48,1024]{2,1,0:T(8,128)(2,1)S(1)}, bf16[3,48,1024]{2,1,0:T(8,128)(2,1)S(1)}, u32[]{:S(2)}, u32[]{:S(2)}) collective-permute-start(bf16[3,48,1024]{2,1,0:T(8,128)(2,1)S(1)} %layer.21.refs_2_.refs_5_), channel_id=1, source_target_pairs={{0,8},{8,16},{16,24},{1,9},{9,17},{17,25},{2,10},{10,18},{18,26},{... | collective-permute-start | bytes 884744 | tf_op jit(solution)/shard_map/ppermute | solution.py:279
  59.4 1.8 %layer.22 = (bf16[3,48,1024]{2,1,0:T(8,128)(2,1)S(1)}, bf16[3,3,48,256]{3,2,1,0:T(8,128)(2,1)S(1)}, bf16[3,3,48,256]{3,2,1,0:T(8,128)(2,1)S(1)}, bf16[3,3,48,256...) custom-call(bf16[3,48,1024]{2,1,0:T(8,128)(2,1)S(1)} %collective-permute-done.14.refs_0_, ...), custom_call_target="tpu_custom_call" | custom-call | flops 301989888 | bytes 7176192 | tf_op jit(solution)/shard_map/layer/pallas_call | solution.py:118
  61.9 3.1 %collective-permute-done.13.refs_0_ = bf16[3,48,1024]{2,1,0:T(8,128)(2,1)S(1)} collective-permute-done((bf16[3,48,1024]{2,1,0:T(8,128)(2,1)S(1)}, bf16[3,48,1024]{2,1,0:T(8,128)(2,1)S(1)}, u32[]{:S(2)}, u32[]{:S(2)}) %collective-permute-start.13) | collective-permute-done | bytes 294944 | tf_op jit(solution)/shard_map/ppermute | solution.py:279
  71.9 1.8 %layer.25 = (bf16[3,48,1024]{2,1,0:T(8,128)(2,1)S(1)}, bf16[3,3,48,256]{3,2,1,0:T(8,128)(2,1)S(1)}, bf16[3,3,48,256]{3,2,1,0:T(8,128)(2,1)S(1)}, bf16[3,3,48,256...) custom-call(bf16[3,48,1024]{2,1,0:T(8,128)(2,1)S(1)} %collective-permute-done.15.refs_0_, ...), custom_call_target="tpu_custom_call" | custom-call | flops 301989888 | bytes 7176192 | tf_op jit(solution)/shard_map/layer/pallas_call | solution.py:118
  75.1 8.2 %collective-permute-done.19.refs_0_ = bf16[3,3,48,256]{3,2,1,0:T(8,128)(2,1)S(1)} collective-permute-done((bf16[3,3,48,256]{3,2,1,0:T(8,128)(2,1)S(1)}, bf16[3,3,48,256]{3,2,1,0:T(8,128)(2,1)S(1)}, u32[]{:S(2)}, u32[]{:S(2)}) %collective-permute-start.19) | collective-permute-done | bytes 221216 | tf_op jit(solution)/shard_map/ppermute | solution.py:249
  89.1 10.1 %collective-permute-done.22.refs_4_ = bf16[3,3,48,256]{3,2,1,0:T(8,128)(2,1)S(1)} collective-permute-done((bf16[3,3,48,256]{3,2,1,0:T(8,128)(2,1)S(1)}, bf16[3,3,48,256]{3,2,1,0:T(8,128)(2,1)S(1)}, u32[]{:S(2)}, u32[]{:S(2)}) %collective-permute-start.22) | collective-permute-done | bytes 221216 | tf_op jit(solution)/shard_map/ppermute | solution.py:249
  103.9 6.5 %collective-permute-start.27 = (bf16[3,48,256]{2,1,0:T(8,128)(2,1)S(1)}, bf16[3,48,256]{2,1,0:T(8,128)(2,1)S(1)}, u32[]{:S(2)}, u32[]{:S(2)}) collective-permute-start(bf16[3,48,256]{2,1,0:T(8,128)(2,1)S(1)} %get-tuple-element.64), channel_id=1, source_target_pairs={{0,3},{1,2},{2,1},{3,0},{4,7},{5,6},{6,5},{7,4},{8,11},{9,10},{10,... | collective-permute-start | bytes 221192 | tf_op jit(solution)/shard_map/ppermute | solution.py:233
  117.7 4.5 %collective-permute-done.34.refs_5_ = bf16[1,3,48,256]{3,2,1,0:T(8,128)(2,1)S(1)} collective-permute-done((bf16[1,3,48,256]{3,2,1,0:T(8,128)(2,1)S(1)}, bf16[1,3,48,256]{3,2,1,0:T(8,128)(2,1)S(1)}, u32[]{:S(2)}, u32[]{:S(2)}) %collective-permute-start.34) | collective-permute-done | bytes 73760 | tf_op jit(solution)/shard_map/ppermute | solution.py:249
  (84 shorter events, 41.0 us)
Async XLA Ops:
  3.4 13.2 %collective-permute-start = (bf16[3,48,1024]{2,1,0:T(8,128)(2,1)S(1)}, bf16[3,48,1024]{2,1,0:T(8,128)(2,1)S(1)}, u32[]{:S(2)}, u32[]{:S(2)}) collective-permute-start(bf16[3,48,1024]{2,1,0:T(8,128)(2,1)S(1)} %get-tuple-element.40), channel_id=1, source_target_pairs={{0,1},{1,0},{2,3},{3,2},{4,5},{5,4},{6,7},{7,6}} | collective-permute-start | bytes 884744 | tf_op jit(solution)/shard_map/ppermute | solution.py:240
  7.6 15.7 %collective-permute-start.6 = (bf16[3,48,1024]{2,1,0:T(8,128)(2,1)S(1)}, bf16[3,48,1024]{2,1,0:T(8,128)(2,1)S(1)}, u32[]{:S(2)}, u32[]{:S(2)}) collective-permute-start(bf16[3,48,1024]{2,1,0:T(8,128)(2,1)S(1)} %layer.14.refs_3_), channel_id=1, source_target_pairs={{0,8},{1,9},{2,10},{3,11},{4,12},{5,13},{6,14},{7,15}} | collective-permute-start | bytes 884744 | tf_op jit(solution)/shard_map/ppermute | solution.py:279
  10.8 12.4 %collective-permute-start.5 = (bf16[3,48,1024]{2,1,0:T(8,128)(2,1)S(1)}, bf16[3,48,1024]{2,1,0:T(8,128)(2,1)S(1)}, u32[]{:S(2)}, u32[]{:S(2)}) collective-permute-start(bf16[3,48,1024]{2,1,0:T(8,128)(2,1)S(1)} %get-tuple-element.46), channel_id=1, source_target_pairs={{0,4},{1,5},{2,6},{3,7},{4,0},{5,1},{6,2},{7,3}} | collective-permute-start | bytes 884744 | tf_op jit(solution)/shard_map/ppermute | solution.py:240
  14.3 15.5 %collective-permute-start.3 = (bf16[3,48,1024]{2,1,0:T(8,128)(2,1)S(1)}, bf16[3,48,1024]{2,1,0:T(8,128)(2,1)S(1)}, u32[]{:S(2)}, u32[]{:S(2)}) collective-permute-start(bf16[3,48,1024]{2,1,0:T(8,128)(2,1)S(1)} %get-tuple-element.45), channel_id=1, source_target_pairs={{0,3},{1,2},{2,1},{3,0},{4,7},{5,6},{6,5},{7,4}} | collective-permute-start | bytes 884744 | tf_op jit(solution)/shard_map/ppermute | solution.py:240
  18.3 11.5 %collective-permute-start.4 = (bf16[3,48,1024]{2,1,0:T(8,128)(2,1)S(1)}, bf16[3,48,1024]{2,1,0:T(8,128)(2,1)S(1)}, u32[]{:S(2)}, u32[]{:S(2)}) collective-permute-start(bf16[3,48,1024]{2,1,0:T(8,128)(2,1)S(1)} %layer.15.token), channel_id=1, source_target_pairs={{0,8},{1,9},{2,10},{3,11},{4,12},{5,13},{6,14},{7,15}} | collective-permute-start | bytes 884744 | tf_op jit(solution)/shard_map/ppermute | solution.py:279
  19.6 15.9 %collective-permute-start.8 = (bf16[3,48,1024]{2,1,0:T(8,128)(2,1)S(1)}, bf16[3,48,1024]{2,1,0:T(8,128)(2,1)S(1)}, u32[]{:S(2)}, u32[]{:S(2)}) collective-permute-start(bf16[3,48,1024]{2,1,0:T(8,128)(2,1)S(1)} %get-tuple-element.47), channel_id=1, source_target_pairs={{0,5},{1,4},{2,7},{3,6},{4,1},{5,0},{6,3},{7,2}} | collective-permute-start | bytes 884744 | tf_op jit(solution)/shard_map/ppermute | solution.py:240
  25.0 10.4 %collective-permute-start.9 = (bf16[3,48,1024]{2,1,0:T(8,128)(2,1)S(1)}, bf16[3,48,1024]{2,1,0:T(8,128)(2,1)S(1)}, u32[]{:S(2)}, u32[]{:S(2)}) collective-permute-start(bf16[3,48,1024]{2,1,0:T(8,128)(2,1)S(1)} %layer.16.refs_4_), channel_id=1, source_target_pairs={{0,8},{8,16},{1,9},{9,17},{2,10},{10,18},{3,11},{11,19},{4,12},{12... | collective-permute-start | bytes 884744 | tf_op jit(solution)/shard_map/ppermute | solution.py:279
  26.3 16.1 %collective-permute-start.2 = (bf16[3,48,1024]{2,1,0:T(8,128)(2,1)S(1)}, bf16[3,48,1024]{2,1,0:T(8,128)(2,1)S(1)}, u32[]{:S(2)}, u32[]{:S(2)}) collective-permute-start(bf16[3,48,1024]{2,1,0:T(8,128)(2,1)S(1)} %get-tuple-element.44), channel_id=1, source_target_pairs={{0,6},{1,7},{2,4},{3,5},{4,2},{5,3},{6,0},{7,1}} | collective-permute-start | bytes 884744 | tf_op jit(solution)/shard_map/ppermute | solution.py:240
  31.6 10.9 %collective-permute-start.7 = (bf16[3,48,1024]{2,1,0:T(8,128)(2,1)S(1)}, bf16[3,48,1024]{2,1,0:T(8,128)(2,1)S(1)}, u32[]{:S(2)}, u32[]{:S(2)}) collective-permute-start(bf16[3,48,1024]{2,1,0:T(8,128)(2,1)S(1)} %layer.17.refs_4_), channel_id=1, source_target_pairs={{0,8},{8,16},{1,9},{9,17},{2,10},{10,18},{3,11},{11,19},{4,12},{12... | collective-permute-start | bytes 884744 | tf_op jit(solution)/shard_map/ppermute | solution.py:279
  32.9 12.9 %collective-permute-start.11 = (bf16[3,48,1024]{2,1,0:T(8,128)(2,1)S(1)}, bf16[3,48,1024]{2,1,0:T(8,128)(2,1)S(1)}, u32[]{:S(2)}, u32[]{:S(2)}) collective-permute-start(bf16[3,48,1024]{2,1,0:T(8,128)(2,1)S(1)} %get-tuple-element.48), channel_id=1, source_target_pairs={{0,7},{1,6},{2,5},{3,4},{4,3},{5,2},{6,1},{7,0}} | collective-permute-start | bytes 884744 | tf_op jit(solution)/shard_map/ppermute | solution.py:240
  39.7 13.2 %collective-permute-start.1 = (bf16[3,48,1024]{2,1,0:T(8,128)(2,1)S(1)}, bf16[3,48,1024]{2,1,0:T(8,128)(2,1)S(1)}, u32[]{:S(2)}, u32[]{:S(2)}) collective-permute-start(bf16[3,48,1024]{2,1,0:T(8,128)(2,1)S(1)} %get-tuple-element.43), channel_id=1, source_target_pairs={{0,2},{1,3},{2,0},{3,1},{4,6},{5,7},{6,4},{7,5}} | collective-permute-start | bytes 884744 | tf_op jit(solution)/shard_map/ppermute | solution.py:240
  48.5 10.9 %collective-permute-start.14 = (bf16[3,48,1024]{2,1,0:T(8,128)(2,1)S(1)}, bf16[3,48,1024]{2,1,0:T(8,128)(2,1)S(1)}, u32[]{:S(2)}, u32[]{:S(2)}) collective-permute-start(bf16[3,48,1024]{2,1,0:T(8,128)(2,1)S(1)} %layer.20.refs_4_.refs_1_), channel_id=1, source_target_pairs={{0,8},{8,16},{16,24},{1,9},{9,17},{17,25},{2,10},{10,18},{18,26},{... | collective-permute-start | bytes 884744 | tf_op jit(solution)/shard_map/ppermute | solution.py:279
  54.9 10.2 %collective-permute-start.13 = (bf16[3,48,1024]{2,1,0:T(8,128)(2,1)S(1)}, bf16[3,48,1024]{2,1,0:T(8,128)(2,1)S(1)}, u32[]{:S(2)}, u32[]{:S(2)}) collective-permute-start(bf16[3,48,1024]{2,1,0:T(8,128)(2,1)S(1)} %layer.21.refs_2_.refs_5_), channel_id=1, source_target_pairs={{0,8},{8,16},{16,24},{1,9},{9,17},{17,25},{2,10},{10,18},{18,26},{... | collective-permute-start | bytes 884744 | tf_op jit(solution)/shard_map/ppermute | solution.py:279
  69.2 16.1 %collective-permute-start.18 = (bf16[3,48,1024]{2,1,0:T(8,128)(2,1)S(1)}, bf16[3,48,1024]{2,1,0:T(8,128)(2,1)S(1)}, u32[]{:S(2)}, u32[]{:S(2)}) collective-permute-start(bf16[3,48,1024]{2,1,0:T(8,128)(2,1)S(1)} %layer.24.refs_2_.refs_5_), channel_id=1, source_target_pairs={{16,24},{17,25},{18,26},{19,27},{20,28},{21,29},{22,30},{23,31}} | collective-permute-start | bytes 884744 | tf_op jit(solution)/shard_map/ppermute | solution.py:279
  69.9 13.4 %collective-permute-start.19 = (bf16[3,3,48,256]{3,2,1,0:T(8,128)(2,1)S(1)}, bf16[3,3,48,256]{3,2,1,0:T(8,128)(2,1)S(1)}, u32[]{:S(2)}, u32[]{:S(2)}) collective-permute-start(bf16[3,3,48,256]{3,2,1,0:T(8,128)(2,1)S(1)} %get-tuple-element.53), channel_id=1, source_target_pairs={{24,0},{25,1},{26,2},{27,3},{28,4},{29,5},{30,6},{31,7}} | collective-permute-start | bytes 663560 | tf_op jit(solution)/shard_map/ppermute | solution.py:249
  71.2 13.4 %collective-permute-start.20 = (bf16[3,3,48,256]{3,2,1,0:T(8,128)(2,1)S(1)}, bf16[3,3,48,256]{3,2,1,0:T(8,128)(2,1)S(1)}, u32[]{:S(2)}, u32[]{:S(2)}) collective-permute-start(bf16[3,3,48,256]{3,2,1,0:T(8,128)(2,1)S(1)} %get-tuple-element.54), channel_id=1, source_target_pairs={{24,8},{25,9},{26,10},{27,11},{28,12},{29,13},{30,14},{31,15}} | collective-permute-start | bytes 663560 | tf_op jit(solution)/shard_map/ppermute | solution.py:249
  73.8 26.1 %collective-permute-start.17 = (bf16[3,48,1024]{2,1,0:T(8,128)(2,1)S(1)}, bf16[3,48,1024]{2,1,0:T(8,128)(2,1)S(1)}, u32[]{:S(2)}, u32[]{:S(2)}) collective-permute-start(bf16[3,48,1024]{2,1,0:T(8,128)(2,1)S(1)} %get-tuple-element.50.refs_3_), channel_id=1, source_target_pairs={{16,24},{17,25},{18,26},{19,27},{20,28},{21,29},{22,30},{23,31}} | collective-permute-start | bytes 884744 | tf_op jit(solution)/shard_map/ppermute | solution.py:279
  74.4 13.3 %collective-permute-start.21 = (bf16[3,3,48,256]{3,2,1,0:T(8,128)(2,1)S(1)}, bf16[3,3,48,256]{3,2,1,0:T(8,128)(2,1)S(1)}, u32[]{:S(2)}, u32[]{:S(2)}) collective-permute-start(bf16[3,3,48,256]{3,2,1,0:T(8,128)(2,1)S(1)} %get-tuple-element.55), channel_id=1, source_target_pairs={{24,16},{25,17},{26,18},{27,19},{28,20},{29,21},{30,22},{31,23}} | collective-permute-start | bytes 663560 | tf_op jit(solution)/shard_map/ppermute | solution.py:249
  83.4 15.8 %collective-permute-start.22 = (bf16[3,3,48,256]{3,2,1,0:T(8,128)(2,1)S(1)}, bf16[3,3,48,256]{3,2,1,0:T(8,128)(2,1)S(1)}, u32[]{:S(2)}, u32[]{:S(2)}) collective-permute-start(bf16[3,3,48,256]{3,2,1,0:T(8,128)(2,1)S(1)} %get-tuple-element.57), channel_id=1, source_target_pairs={{24,0},{25,1},{26,2},{27,3},{28,4},{29,5},{30,6},{31,7}} | collective-permute-start | bytes 663560 | tf_op jit(solution)/shard_map/ppermute | solution.py:249
  84.7 17.7 %collective-permute-start.23 = (bf16[3,3,48,256]{3,2,1,0:T(8,128)(2,1)S(1)}, bf16[3,3,48,256]{3,2,1,0:T(8,128)(2,1)S(1)}, u32[]{:S(2)}, u32[]{:S(2)}) collective-permute-start(bf16[3,3,48,256]{3,2,1,0:T(8,128)(2,1)S(1)} %get-tuple-element.58), channel_id=1, source_target_pairs={{24,8},{25,9},{26,10},{27,11},{28,12},{29,13},{30,14},{31,15}} | collective-permute-start | bytes 663560 | tf_op jit(solution)/shard_map/ppermute | solution.py:249
  85.3 17.0 %collective-permute-start.24 = (bf16[3,3,48,256]{3,2,1,0:T(8,128)(2,1)S(1)}, bf16[3,3,48,256]{3,2,1,0:T(8,128)(2,1)S(1)}, u32[]{:S(2)}, u32[]{:S(2)}) collective-permute-start(bf16[3,3,48,256]{3,2,1,0:T(8,128)(2,1)S(1)} %get-tuple-element.59), channel_id=1, source_target_pairs={{24,16},{25,17},{26,18},{27,19},{28,20},{29,21},{30,22},{31,23}} | collective-permute-start | bytes 663560 | tf_op jit(solution)/shard_map/ppermute | solution.py:249
  87.8 16.2 %collective-permute-start.30 = (bf16[1,3,48,256]{3,2,1,0:T(8,128)(2,1)S(1)}, bf16[1,3,48,256]{3,2,1,0:T(8,128)(2,1)S(1)}, u32[]{:S(2)}, u32[]{:S(2)}) collective-permute-start(bf16[1,3,48,256]{3,2,1,0:T(8,128)(2,1)S(1)} %get-tuple-element.51.refs_3_), channel_id=1, source_target_pairs={{24,7},{25,6},{26,5},{27,4},{28,3},{29,2},{30,1},{31,0}} | collective-permute-start | bytes 221192 | tf_op jit(solution)/shard_map/ppermute | solution.py:249
  99.2 11.3 %collective-permute-start.31 = (bf16[1,3,48,256]{3,2,1,0:T(8,128)(2,1)S(1)}, bf16[1,3,48,256]{3,2,1,0:T(8,128)(2,1)S(1)}, u32[]{:S(2)}, u32[]{:S(2)}) collective-permute-start(bf16[1,3,48,256]{3,2,1,0:T(8,128)(2,1)S(1)} %get-tuple-element.67), channel_id=1, source_target_pairs={{24,15},{25,14},{26,13},{27,12},{28,11},{29,10},{30,9},{31,8}} | collective-permute-start | bytes 221192 | tf_op jit(solution)/shard_map/ppermute | solution.py:249
  99.9 10.6 %collective-permute-start.32 = (bf16[1,3,48,256]{3,2,1,0:T(8,128)(2,1)S(1)}, bf16[1,3,48,256]{3,2,1,0:T(8,128)(2,1)S(1)}, u32[]{:S(2)}, u32[]{:S(2)}) collective-permute-start(bf16[1,3,48,256]{3,2,1,0:T(8,128)(2,1)S(1)} %get-tuple-element.68), channel_id=1, source_target_pairs={{24,23},{25,22},{26,21},{27,20},{28,19},{29,18},{30,17},{31,16}} | collective-permute-start | bytes 221192 | tf_op jit(solution)/shard_map/ppermute | solution.py:249
  (20 other events, 117.4 us)

commit v3 on v2

--- a/solution.py
+++ b/solution.py
@@ -237,7 +237,12 @@
     def arriving(x, i):
         if i == 0:
             return x
-        return lax.ppermute(x, ("section", "rep"), [(d, d ^ i) for d in range(rep_count)])
+        hops = [
+            (s * rep_count + d, s * rep_count + (d ^ (i if s == 0 else 1)))
+            for s in range(section_count)
+            for d in range(rep_count)
+        ]
+        return lax.ppermute(x, ("section", "rep"), hops)
 
     entering = {i: arriving(outgoing[i], i) for i in order}
 
@@ -246,6 +251,12 @@
         for s, piece in enumerate(pieces):
             if s != last or hop != 0:
                 hops = [(last * rep_count + d, s * rep_count + (d ^ hop)) for d in range(rep_count)]
+                if s == last:
+                    hops += [
+                        (t * rep_count + d, t * rep_count + (d ^ 1))
+                        for t in range(last)
+                        for d in range(rep_count)
+                    ]
                 piece = lax.ppermute(piece, ("section", "rep"), hops)
             sent.append(piece)
         return sent
@@ -304,7 +315,9 @@
         name="pick",
     )(token, *[piece for group in groups for piece in back[group[0]]])
     early = order[: len(mine)]
-    returned = [traded(piece, i) for i, piece in zip(early, mine)]
+    returned = []
+    for i, piece in zip(early, mine):
+        returned.append(traded(piece, i))
 
     def combined(these, acc, given, dtype, is_direct):
         spans = [(i * chunk_rows, (i + 1) * chunk_rows) for i in these]

time: 124 us -> 119 us (0.960)
  starting transfers between devices: 64 us -> 56.1 us
  waiting for transfers between devices: 28.6 us -> 31.8 us
    ppermute x7, starting transfers between devices: 20.1 us -> 9.7 us  [arriving(): return lax.ppermute(x, ('section', 'rep'), hops)]
    ppermute x12, starting transfers between devices: 22.7 us -> 26.9 us  [on_device(): inbound[n + STREAMS] = lax.ppermute(made[0], 'section', forward)]
    ppermute x7, waiting for transfers between devices: 0.02 us -> 2.53 us  [arriving(): return lax.ppermute(x, ('section', 'rep'), hops)]
    ppermute x5, starting transfers between devices: 9.44 us -> 7.69 us  [traded(): return lax.ppermute(x, 'rep', [(d, d ^ i) for d in range(rep_count)])]
  transfers between devices with their start and end apart: 38 -> 38, of which waited for: 8 -> 10; matrix products, arithmetic and copies ran while one was open for 0% -> 0% of each run, Pallas kernels for 21% -> 22%
where the time goes in v3:
time: 119 us; the launch traced here: 118 us
  starting transfers between devices  56.1 us (47%)
  waiting for transfers between devices  31.8 us (27%)
  Pallas kernels  28.7 us (24%)
  local copies, waits for them, and re-layouts  1.24 us (1%)
    ppermute x12, starting transfers between devices, on_device(): inbound[n + STREAMS] = lax.ppermute(made[0], 'section', forward)  26.9 us
    pallas_call x14, Pallas kernels, layer(): pl.pallas_call(functools.partial(layer_kernel, first is not None, arrived...  24.5 us
    ppermute x14, waiting for transfers between devices, sent_back(): piece = lax.ppermute(piece, ('section', 'rep'), hops)  23.2 us
    ppermute x14, starting transfers between devices, sent_back(): piece = lax.ppermute(piece, ('section', 'rep'), hops)  11.8 us
    ppermute x7, starting transfers between devices, arriving(): return lax.ppermute(x, ('section', 'rep'), hops)  9.7 us
    ppermute x5, starting transfers between devices, traded(): return lax.ppermute(x, 'rep', [(d, d ^ i) for d in range(rep_count)])  7.69 us
    ppermute x12, waiting for transfers between devices, on_device(): inbound[n + STREAMS] = lax.ppermute(made[0], 'section', forward)  4.68 us
    ppermute x7, waiting for transfers between devices, arriving(): return lax.ppermute(x, ('section', 'rep'), hops)  2.53 us
  transfers between devices with their start and end apart: 38, of which 10 were waited for; matrix products, arithmetic and copies ran while one was open for 0% of the time, Pallas kernels for 22%

profile of v3, /device:TPU:0, one launch (start us, length us, event | category | flops | bytes accessed | tf_op | source)
XLA Modules:
  0.0 118.3 jit_solution(18085858331011253808)
XLA Ops:
  1.3 2.1 %dispatch.1 = (s32[4,1,128]{2,1,0:T(1,128)S(1)}, f32[3,2,1024]{2,1,0:T(2,128)S(1)}, bf16[3,48,1024]{2,1,0:T(8,128)(2,1)S(1)}, bf16[3,48,1024]{2,1,0:T(8,128)(2,1...) custom-call(s32[16]{0:T(128)S(1)} %copy-done.4, ...), custom_call_target="tpu_custom_call" | custom-call | flops 1207959552 | bytes 3407872 | tf_op jit(solution)/shard_map/dispatch/pallas_call | solution.py:210
  5.7 4.5 %collective-permute-start.6 = (bf16[3,48,1024]{2,1,0:T(8,128)(2,1)S(1)}, bf16[3,48,1024]{2,1,0:T(8,128)(2,1)S(1)}, u32[]{:S(2)}, u32[]{:S(2)}) collective-permute-start(bf16[3,48,1024]{2,1,0:T(8,128)(2,1)S(1)} %layer.14.refs_3_), channel_id=1, source_target_pairs={{0,8},{1,9},{2,10},{3,11},{4,12},{5,13},{6,14},{7,15}} | collective-permute-start | bytes 884744 | tf_op jit(solution)/shard_map/ppermute | solution.py:290
  17.3 2.5 %collective-permute-done.5.refs_0_ = bf16[3,48,1024]{2,1,0:T(8,128)(2,1)S(1)} collective-permute-done((bf16[3,48,1024]{2,1,0:T(8,128)(2,1)S(1)}, bf16[3,48,1024]{2,1,0:T(8,128)(2,1)S(1)}, u32[]{:S(2)}, u32[]{:S(2)}) %collective-permute-start.5) | collective-permute-done | bytes 294944 | tf_op jit(solution)/shard_map/ppermute | solution.py:245
  19.8 1.7 %layer.16.refs_4_ = bf16[3,48,1024]{2,1,0:T(8,128)(2,1)S(1)} custom-call(bf16[3,48,1024]{2,1,0:T(8,128)(2,1)S(1)} %collective-permute-done.5.refs_0_, bf16[3,48,1024]{2,1,0:T(8,128)(2,1)S(1)} %collective-permute-done.6.refs_1_, f32[3,2,1024]{2,1,0:T(2,128)S(1)} %get-tuple-element.41.refs_1_.refs_2_.refs_3_, bf16[3,1024,1024]{2,1,0:T(8,128)(2,1)S(1)} %bitcast.5, ...), custom_call_target="tpu_custom_call" | custom-call | flops 301989888 | bytes 7176192 | tf_op jit(solution)/shard_map/layer/pallas_call | solution.py:118
  21.6 1.9 %collective-permute-start.9 = (bf16[3,48,1024]{2,1,0:T(8,128)(2,1)S(1)}, bf16[3,48,1024]{2,1,0:T(8,128)(2,1)S(1)}, u32[]{:S(2)}, u32[]{:S(2)}) collective-permute-start(bf16[3,48,1024]{2,1,0:T(8,128)(2,1)S(1)} %layer.16.refs_4_), channel_id=1, source_target_pairs={{0,8},{8,16},{1,9},{9,17},{2,10},{10,18},{3,11},{11,19},{4,12},{12... | collective-permute-start | bytes 884744 | tf_op jit(solution)/shard_map/ppermute | solution.py:290
  23.5 2.8 %collective-permute-start.2 = (bf16[3,48,1024]{2,1,0:T(8,128)(2,1)S(1)}, bf16[3,48,1024]{2,1,0:T(8,128)(2,1)S(1)}, u32[]{:S(2)}, u32[]{:S(2)}) collective-permute-start(bf16[3,48,1024]{2,1,0:T(8,128)(2,1)S(1)} %get-tuple-element.44), channel_id=1, source_target_pairs={{0,6},{1,7},{2,4},{3,5},{4,2},{5,3},{6,0},{7,1},{8,9},{9,8},{10,11... | collective-permute-start | bytes 884744 | tf_op jit(solution)/shard_map/ppermute | solution.py:245
  28.0 1.8 %collective-permute-start.7 = (bf16[3,48,1024]{2,1,0:T(8,128)(2,1)S(1)}, bf16[3,48,1024]{2,1,0:T(8,128)(2,1)S(1)}, u32[]{:S(2)}, u32[]{:S(2)}) collective-permute-start(bf16[3,48,1024]{2,1,0:T(8,128)(2,1)S(1)} %layer.17.refs_4_), channel_id=1, source_target_pairs={{0,8},{8,16},{1,9},{9,17},{2,10},{10,18},{3,11},{11,19},{4,12},{12... | collective-permute-start | bytes 884744 | tf_op jit(solution)/shard_map/ppermute | solution.py:290
  31.0 1.7 %layer.18.refs_4_ = bf16[3,48,1024]{2,1,0:T(8,128)(2,1)S(1)} custom-call(bf16[3,48,1024]{2,1,0:T(8,128)(2,1)S(1)} %collective-permute-done.8.refs_0_, bf16[3,48,1024]{2,1,0:T(8,128)(2,1)S(1)} %collective-permute-done.9.refs_1_, f32[3,2,1024]{2,1,0:T(2,128)S(1)} %get-tuple-element.41.refs_1_.refs_2_.refs_3_, bf16[3,1024,1024]{2,1,0:T(8,128)(2,1)S(1)} %bitcast.7, ...), custom_call_target="tpu_custom_call" | custom-call | flops 301989888 | bytes 7176192 | tf_op jit(solution)/shard_map/layer/pallas_call | solution.py:118
  32.8 3.3 %collective-permute-start.12 = (bf16[3,48,1024]{2,1,0:T(8,128)(2,1)S(1)}, bf16[3,48,1024]{2,1,0:T(8,128)(2,1)S(1)}, u32[]{:S(2)}, u32[]{:S(2)}) collective-permute-start(bf16[3,48,1024]{2,1,0:T(8,128)(2,1)S(1)} %layer.18.refs_4_), channel_id=1, source_target_pairs={{0,8},{8,16},{16,24},{1,9},{9,17},{17,25},{2,10},{10,18},{18,26},{... | collective-permute-start | bytes 884744 | tf_op jit(solution)/shard_map/ppermute | solution.py:290
  36.1 1.8 %collective-permute-start.1 = (bf16[3,48,1024]{2,1,0:T(8,128)(2,1)S(1)}, bf16[3,48,1024]{2,1,0:T(8,128)(2,1)S(1)}, u32[]{:S(2)}, u32[]{:S(2)}) collective-permute-start(bf16[3,48,1024]{2,1,0:T(8,128)(2,1)S(1)} %get-tuple-element.43), channel_id=1, source_target_pairs={{0,2},{1,3},{2,0},{3,1},{4,6},{5,7},{6,4},{7,5},{8,9},{9,8},{10,11... | collective-permute-start | bytes 884744 | tf_op jit(solution)/shard_map/ppermute | solution.py:245
  39.6 2.5 %collective-permute-start.10 = (bf16[3,48,1024]{2,1,0:T(8,128)(2,1)S(1)}, bf16[3,48,1024]{2,1,0:T(8,128)(2,1)S(1)}, u32[]{:S(2)}, u32[]{:S(2)}) collective-permute-start(bf16[3,48,1024]{2,1,0:T(8,128)(2,1)S(1)} %layer.19.refs_4_), channel_id=1, source_target_pairs={{0,8},{8,16},{16,24},{1,9},{9,17},{17,25},{2,10},{10,18},{18,26},{... | collective-permute-start | bytes 884744 | tf_op jit(solution)/shard_map/ppermute | solution.py:290
  45.2 4.4 %collective-permute-start.14 = (bf16[3,48,1024]{2,1,0:T(8,128)(2,1)S(1)}, bf16[3,48,1024]{2,1,0:T(8,128)(2,1)S(1)}, u32[]{:S(2)}, u32[]{:S(2)}) collective-permute-start(bf16[3,48,1024]{2,1,0:T(8,128)(2,1)S(1)} %layer.20.refs_4_.refs_1_), channel_id=1, source_target_pairs={{0,8},{8,16},{16,24},{1,9},{9,17},{17,25},{2,10},{10,18},{18,26},{... | collective-permute-start | bytes 884744 | tf_op jit(solution)/shard_map/ppermute | solution.py:290
  51.5 4.4 %collective-permute-start.13 = (bf16[3,48,1024]{2,1,0:T(8,128)(2,1)S(1)}, bf16[3,48,1024]{2,1,0:T(8,128)(2,1)S(1)}, u32[]{:S(2)}, u32[]{:S(2)}) collective-permute-start(bf16[3,48,1024]{2,1,0:T(8,128)(2,1)S(1)} %layer.21.refs_2_.refs_5_), channel_id=1, source_target_pairs={{0,8},{8,16},{16,24},{1,9},{9,17},{17,25},{2,10},{10,18},{18,26},{... | collective-permute-start | bytes 884744 | tf_op jit(solution)/shard_map/ppermute | solution.py:290
  56.1 1.8 %layer.22 = (bf16[3,48,1024]{2,1,0:T(8,128)(2,1)S(1)}, bf16[3,3,48,256]{3,2,1,0:T(8,128)(2,1)S(1)}, bf16[3,3,48,256]{3,2,1,0:T(8,128)(2,1)S(1)}, bf16[3,3,48,256...) custom-call(bf16[3,48,1024]{2,1,0:T(8,128)(2,1)S(1)} %collective-permute-done.14.refs_0_, ...), custom_call_target="tpu_custom_call" | custom-call | flops 301989888 | bytes 7176192 | tf_op jit(solution)/shard_map/layer/pallas_call | solution.py:118
  58.6 2.8 %collective-permute-done.13.refs_0_ = bf16[3,48,1024]{2,1,0:T(8,128)(2,1)S(1)} collective-permute-done((bf16[3,48,1024]{2,1,0:T(8,128)(2,1)S(1)}, bf16[3,48,1024]{2,1,0:T(8,128)(2,1)S(1)}, u32[]{:S(2)}, u32[]{:S(2)}) %collective-permute-start.13) | collective-permute-done | bytes 294944 | tf_op jit(solution)/shard_map/ppermute | solution.py:290
  63.8 1.7 %layer.24.refs_2_.refs_5_ = bf16[3,48,1024]{2,1,0:T(8,128)(2,1)S(1)} custom-call(bf16[3,48,1024]{2,1,0:T(8,128)(2,1)S(1)} %collective-permute-done.16.refs_0_, f32[3,2,1024]{2,1,0:T(2,128)S(1)} %get-tuple-element.41.refs_1_.refs_2_.refs_3_, bf16[3,1024,1024]{2,1,0:T(8,128)(2,1)S(1)} %bitcast.13, bf16[3,48,1024]{2,1,0:T(8,128)(2,1)S(1)} %layer.23.refs_3_.refs_1_), custom_call_target="tpu_custom_call" | custom-call | flops 301989888 | bytes 7176192 | tf_op jit(solution)/shard_map/layer/pallas_call | solution.py:118
  68.2 1.8 %layer.25 = (bf16[3,48,1024]{2,1,0:T(8,128)(2,1)S(1)}, bf16[3,3,48,256]{3,2,1,0:T(8,128)(2,1)S(1)}, bf16[3,3,48,256]{3,2,1,0:T(8,128)(2,1)S(1)}, bf16[3,3,48,256...) custom-call(bf16[3,48,1024]{2,1,0:T(8,128)(2,1)S(1)} %collective-permute-done.15.refs_0_, ...), custom_call_target="tpu_custom_call" | custom-call | flops 301989888 | bytes 7176192 | tf_op jit(solution)/shard_map/layer/pallas_call | solution.py:118
  71.4 7.2 %collective-permute-done.19.refs_0_ = bf16[3,3,48,256]{3,2,1,0:T(8,128)(2,1)S(1)} collective-permute-done((bf16[3,3,48,256]{3,2,1,0:T(8,128)(2,1)S(1)}, bf16[3,3,48,256]{3,2,1,0:T(8,128)(2,1)S(1)}, u32[]{:S(2)}, u32[]{:S(2)}) %collective-permute-start.19) | collective-permute-done | bytes 221216 | tf_op jit(solution)/shard_map/ppermute | solution.py:260
  81.3 1.7 %layer.26 = (bf16[1,3,48,256]{3,2,1,0:T(8,128)(2,1)S(1)}, bf16[1,3,48,256]{3,2,1,0:T(8,128)(2,1)S(1)}, bf16[1,3,48,256]{3,2,1,0:T(8,128)(2,1)S(1)}, bf16[1,3,48,256]{3,2,1,0:T(8,128)(2,1)S(1)}) custom-call(bf16[3,48,1024]{2,1,0:T(8,128)(2,1)S(1)} %collective-permute-done.18.refs_0_, f32[3,2,1024]{2,1,0:T(2,128)S(1)} %get-tuple-element.41.refs_1_.refs_2_.refs_3_, ...), custom_call_target="tpu_custom_call" | custom-call | flops 301989888 | bytes 7176192 | tf_op jit(solution)/shard_map/layer/pallas_call | solution.py:118
  84.4 11.3 %collective-permute-done.22.refs_4_ = bf16[3,3,48,256]{3,2,1,0:T(8,128)(2,1)S(1)} collective-permute-done((bf16[3,3,48,256]{3,2,1,0:T(8,128)(2,1)S(1)}, bf16[3,3,48,256]{3,2,1,0:T(8,128)(2,1)S(1)}, u32[]{:S(2)}, u32[]{:S(2)}) %collective-permute-start.22) | collective-permute-done | bytes 221216 | tf_op jit(solution)/shard_map/ppermute | solution.py:260
  97.0 1.7 %layer.27 = (bf16[1,3,48,256]{3,2,1,0:T(8,128)(2,1)S(1)}, bf16[1,3,48,256]{3,2,1,0:T(8,128)(2,1)S(1)}, bf16[1,3,48,256]{3,2,1,0:T(8,128)(2,1)S(1)}, bf16[1,3,48,256]{3,2,1,0:T(8,128)(2,1)S(1)}) custom-call(bf16[3,48,1024]{2,1,0:T(8,128)(2,1)S(1)} %collective-permute-done.17.refs_0_, f32[3,2,1024]{2,1,0:T(2,128)S(1)} %get-tuple-element.41.refs_1_.refs_2_.refs_3_, ...), custom_call_target="tpu_custom_call" | custom-call | flops 301989888 | bytes 7176192 | tf_op jit(solution)/shard_map/layer/pallas_call | solution.py:118
  99.0 2.4 %collective-permute-start.26 = (bf16[3,48,256]{2,1,0:T(8,128)(2,1)S(1)}, bf16[3,48,256]{2,1,0:T(8,128)(2,1)S(1)}, u32[]{:S(2)}, u32[]{:S(2)}) collective-permute-start(bf16[3,48,256]{2,1,0:T(8,128)(2,1)S(1)} %get-tuple-element.63), channel_id=1, source_target_pairs={{0,4},{1,5},{2,6},{3,7},{4,0},{5,1},{6,2},{7,3},{8,12},{9,13},{10,... | collective-permute-start | bytes 221192 | tf_op jit(solution)/shard_map/ppermute | solution.py:233
  101.4 3.8 %collective-permute-start.27 = (bf16[3,48,256]{2,1,0:T(8,128)(2,1)S(1)}, bf16[3,48,256]{2,1,0:T(8,128)(2,1)S(1)}, u32[]{:S(2)}, u32[]{:S(2)}) collective-permute-start(bf16[3,48,256]{2,1,0:T(8,128)(2,1)S(1)} %get-tuple-element.64), channel_id=1, source_target_pairs={{0,3},{1,2},{2,1},{3,0},{4,7},{5,6},{6,5},{7,4},{8,11},{9,10},{10,... | collective-permute-start | bytes 221192 | tf_op jit(solution)/shard_map/ppermute | solution.py:233
  112.5 4.7 %collective-permute-done.34.refs_5_ = bf16[1,3,48,256]{3,2,1,0:T(8,128)(2,1)S(1)} collective-permute-done((bf16[1,3,48,256]{3,2,1,0:T(8,128)(2,1)S(1)}, bf16[1,3,48,256]{3,2,1,0:T(8,128)(2,1)S(1)}, u32[]{:S(2)}, u32[]{:S(2)}) %collective-permute-start.34) | collective-permute-done | bytes 73760 | tf_op jit(solution)/shard_map/ppermute | solution.py:260
  (84 shorter events, 41.3 us)
Async XLA Ops:
  3.4 9.4 %collective-permute-start = (bf16[3,48,1024]{2,1,0:T(8,128)(2,1)S(1)}, bf16[3,48,1024]{2,1,0:T(8,128)(2,1)S(1)}, u32[]{:S(2)}, u32[]{:S(2)}) collective-permute-start(bf16[3,48,1024]{2,1,0:T(8,128)(2,1)S(1)} %get-tuple-element.40), channel_id=1, source_target_pairs={{0,1},{1,0},{2,3},{3,2},{4,5},{5,4},{6,7},{7,6},{8,9},{9,8},{10,11... | collective-permute-start | bytes 884744 | tf_op jit(solution)/shard_map/ppermute | solution.py:245
  5.7 11.6 %collective-permute-start.6 = (bf16[3,48,1024]{2,1,0:T(8,128)(2,1)S(1)}, bf16[3,48,1024]{2,1,0:T(8,128)(2,1)S(1)}, u32[]{:S(2)}, u32[]{:S(2)}) collective-permute-start(bf16[3,48,1024]{2,1,0:T(8,128)(2,1)S(1)} %layer.14.refs_3_), channel_id=1, source_target_pairs={{0,8},{1,9},{2,10},{3,11},{4,12},{5,13},{6,14},{7,15}} | collective-permute-start | bytes 884744 | tf_op jit(solution)/shard_map/ppermute | solution.py:290
  10.2 9.6 %collective-permute-start.5 = (bf16[3,48,1024]{2,1,0:T(8,128)(2,1)S(1)}, bf16[3,48,1024]{2,1,0:T(8,128)(2,1)S(1)}, u32[]{:S(2)}, u32[]{:S(2)}) collective-permute-start(bf16[3,48,1024]{2,1,0:T(8,128)(2,1)S(1)} %get-tuple-element.46), channel_id=1, source_target_pairs={{0,4},{1,5},{2,6},{3,7},{4,0},{5,1},{6,2},{7,3},{8,9},{9,8},{10,11... | collective-permute-start | bytes 884744 | tf_op jit(solution)/shard_map/ppermute | solution.py:245
  11.8 14.5 %collective-permute-start.3 = (bf16[3,48,1024]{2,1,0:T(8,128)(2,1)S(1)}, bf16[3,48,1024]{2,1,0:T(8,128)(2,1)S(1)}, u32[]{:S(2)}, u32[]{:S(2)}) collective-permute-start(bf16[3,48,1024]{2,1,0:T(8,128)(2,1)S(1)} %get-tuple-element.45), channel_id=1, source_target_pairs={{0,3},{1,2},{2,1},{3,0},{4,7},{5,6},{6,5},{7,4},{8,9},{9,8},{10,11... | collective-permute-start | bytes 884744 | tf_op jit(solution)/shard_map/ppermute | solution.py:245
  14.5 11.7 %collective-permute-start.4 = (bf16[3,48,1024]{2,1,0:T(8,128)(2,1)S(1)}, bf16[3,48,1024]{2,1,0:T(8,128)(2,1)S(1)}, u32[]{:S(2)}, u32[]{:S(2)}) collective-permute-start(bf16[3,48,1024]{2,1,0:T(8,128)(2,1)S(1)} %layer.15.token), channel_id=1, source_target_pairs={{0,8},{1,9},{2,10},{3,11},{4,12},{5,13},{6,14},{7,15}} | collective-permute-start | bytes 884744 | tf_op jit(solution)/shard_map/ppermute | solution.py:290
  15.9 15.1 %collective-permute-start.8 = (bf16[3,48,1024]{2,1,0:T(8,128)(2,1)S(1)}, bf16[3,48,1024]{2,1,0:T(8,128)(2,1)S(1)}, u32[]{:S(2)}, u32[]{:S(2)}) collective-permute-start(bf16[3,48,1024]{2,1,0:T(8,128)(2,1)S(1)} %get-tuple-element.47), channel_id=1, source_target_pairs={{0,5},{1,4},{2,7},{3,6},{4,1},{5,0},{6,3},{7,2},{8,9},{9,8},{10,11... | collective-permute-start | bytes 884744 | tf_op jit(solution)/shard_map/ppermute | solution.py:245
  23.5 14.4 %collective-permute-start.2 = (bf16[3,48,1024]{2,1,0:T(8,128)(2,1)S(1)}, bf16[3,48,1024]{2,1,0:T(8,128)(2,1)S(1)}, u32[]{:S(2)}, u32[]{:S(2)}) collective-permute-start(bf16[3,48,1024]{2,1,0:T(8,128)(2,1)S(1)} %get-tuple-element.44), channel_id=1, source_target_pairs={{0,6},{1,7},{2,4},{3,5},{4,2},{5,3},{6,0},{7,1},{8,9},{9,8},{10,11... | collective-permute-start | bytes 884744 | tf_op jit(solution)/shard_map/ppermute | solution.py:245
  28.0 9.9 %collective-permute-start.7 = (bf16[3,48,1024]{2,1,0:T(8,128)(2,1)S(1)}, bf16[3,48,1024]{2,1,0:T(8,128)(2,1)S(1)}, u32[]{:S(2)}, u32[]{:S(2)}) collective-permute-start(bf16[3,48,1024]{2,1,0:T(8,128)(2,1)S(1)} %layer.17.refs_4_), channel_id=1, source_target_pairs={{0,8},{8,16},{1,9},{9,17},{2,10},{10,18},{3,11},{11,19},{4,12},{12... | collective-permute-start | bytes 884744 | tf_op jit(solution)/shard_map/ppermute | solution.py:290
  29.8 12.4 %collective-permute-start.11 = (bf16[3,48,1024]{2,1,0:T(8,128)(2,1)S(1)}, bf16[3,48,1024]{2,1,0:T(8,128)(2,1)S(1)}, u32[]{:S(2)}, u32[]{:S(2)}) collective-permute-start(bf16[3,48,1024]{2,1,0:T(8,128)(2,1)S(1)} %get-tuple-element.48), channel_id=1, source_target_pairs={{0,7},{1,6},{2,5},{3,4},{4,3},{5,2},{6,1},{7,0},{8,9},{9,8},{10,11... | collective-permute-start | bytes 884744 | tf_op jit(solution)/shard_map/ppermute | solution.py:245
  32.8 10.7 %collective-permute-start.12 = (bf16[3,48,1024]{2,1,0:T(8,128)(2,1)S(1)}, bf16[3,48,1024]{2,1,0:T(8,128)(2,1)S(1)}, u32[]{:S(2)}, u32[]{:S(2)}) collective-permute-start(bf16[3,48,1024]{2,1,0:T(8,128)(2,1)S(1)} %layer.18.refs_4_), channel_id=1, source_target_pairs={{0,8},{8,16},{16,24},{1,9},{9,17},{17,25},{2,10},{10,18},{18,26},{... | collective-permute-start | bytes 884744 | tf_op jit(solution)/shard_map/ppermute | solution.py:290
  36.1 13.5 %collective-permute-start.1 = (bf16[3,48,1024]{2,1,0:T(8,128)(2,1)S(1)}, bf16[3,48,1024]{2,1,0:T(8,128)(2,1)S(1)}, u32[]{:S(2)}, u32[]{:S(2)}) collective-permute-start(bf16[3,48,1024]{2,1,0:T(8,128)(2,1)S(1)} %get-tuple-element.43), channel_id=1, source_target_pairs={{0,2},{1,3},{2,0},{3,1},{4,6},{5,7},{6,4},{7,5},{8,9},{9,8},{10,11... | collective-permute-start | bytes 884744 | tf_op jit(solution)/shard_map/ppermute | solution.py:245
  39.6 10.1 %collective-permute-start.10 = (bf16[3,48,1024]{2,1,0:T(8,128)(2,1)S(1)}, bf16[3,48,1024]{2,1,0:T(8,128)(2,1)S(1)}, u32[]{:S(2)}, u32[]{:S(2)}) collective-permute-start(bf16[3,48,1024]{2,1,0:T(8,128)(2,1)S(1)} %layer.19.refs_4_), channel_id=1, source_target_pairs={{0,8},{8,16},{16,24},{1,9},{9,17},{17,25},{2,10},{10,18},{18,26},{... | collective-permute-start | bytes 884744 | tf_op jit(solution)/shard_map/ppermute | solution.py:290
  45.2 10.9 %collective-permute-start.14 = (bf16[3,48,1024]{2,1,0:T(8,128)(2,1)S(1)}, bf16[3,48,1024]{2,1,0:T(8,128)(2,1)S(1)}, u32[]{:S(2)}, u32[]{:S(2)}) collective-permute-start(bf16[3,48,1024]{2,1,0:T(8,128)(2,1)S(1)} %layer.20.refs_4_.refs_1_), channel_id=1, source_target_pairs={{0,8},{8,16},{16,24},{1,9},{9,17},{17,25},{2,10},{10,18},{18,26},{... | collective-permute-start | bytes 884744 | tf_op jit(solution)/shard_map/ppermute | solution.py:290
  51.5 9.9 %collective-permute-start.13 = (bf16[3,48,1024]{2,1,0:T(8,128)(2,1)S(1)}, bf16[3,48,1024]{2,1,0:T(8,128)(2,1)S(1)}, u32[]{:S(2)}, u32[]{:S(2)}) collective-permute-start(bf16[3,48,1024]{2,1,0:T(8,128)(2,1)S(1)} %layer.21.refs_2_.refs_5_), channel_id=1, source_target_pairs={{0,8},{8,16},{16,24},{1,9},{9,17},{17,25},{2,10},{10,18},{18,26},{... | collective-permute-start | bytes 884744 | tf_op jit(solution)/shard_map/ppermute | solution.py:290
  65.5 15.1 %collective-permute-start.18 = (bf16[3,48,1024]{2,1,0:T(8,128)(2,1)S(1)}, bf16[3,48,1024]{2,1,0:T(8,128)(2,1)S(1)}, u32[]{:S(2)}, u32[]{:S(2)}) collective-permute-start(bf16[3,48,1024]{2,1,0:T(8,128)(2,1)S(1)} %layer.24.refs_2_.refs_5_), channel_id=1, source_target_pairs={{16,24},{17,25},{18,26},{19,27},{20,28},{21,29},{22,30},{23,31}} | collective-permute-start | bytes 884744 | tf_op jit(solution)/shard_map/ppermute | solution.py:290
  66.2 12.4 %collective-permute-start.19 = (bf16[3,3,48,256]{3,2,1,0:T(8,128)(2,1)S(1)}, bf16[3,3,48,256]{3,2,1,0:T(8,128)(2,1)S(1)}, u32[]{:S(2)}, u32[]{:S(2)}) collective-permute-start(bf16[3,3,48,256]{3,2,1,0:T(8,128)(2,1)S(1)} %get-tuple-element.53), channel_id=1, source_target_pairs={{24,0},{25,1},{26,2},{27,3},{28,4},{29,5},{30,6},{31,7}} | collective-permute-start | bytes 663560 | tf_op jit(solution)/shard_map/ppermute | solution.py:260
  67.5 12.4 %collective-permute-start.20 = (bf16[3,3,48,256]{3,2,1,0:T(8,128)(2,1)S(1)}, bf16[3,3,48,256]{3,2,1,0:T(8,128)(2,1)S(1)}, u32[]{:S(2)}, u32[]{:S(2)}) collective-permute-start(bf16[3,3,48,256]{3,2,1,0:T(8,128)(2,1)S(1)} %get-tuple-element.54), channel_id=1, source_target_pairs={{24,8},{25,9},{26,10},{27,11},{28,12},{29,13},{30,14},{31,15}} | collective-permute-start | bytes 663560 | tf_op jit(solution)/shard_map/ppermute | solution.py:260
  70.0 26.3 %collective-permute-start.17 = (bf16[3,48,1024]{2,1,0:T(8,128)(2,1)S(1)}, bf16[3,48,1024]{2,1,0:T(8,128)(2,1)S(1)}, u32[]{:S(2)}, u32[]{:S(2)}) collective-permute-start(bf16[3,48,1024]{2,1,0:T(8,128)(2,1)S(1)} %get-tuple-element.50.refs_3_), channel_id=1, source_target_pairs={{16,24},{17,25},{18,26},{19,27},{20,28},{21,29},{22,30},{23,31}} | collective-permute-start | bytes 884744 | tf_op jit(solution)/shard_map/ppermute | solution.py:290
  70.7 12.3 %collective-permute-start.21 = (bf16[3,3,48,256]{3,2,1,0:T(8,128)(2,1)S(1)}, bf16[3,3,48,256]{3,2,1,0:T(8,128)(2,1)S(1)}, u32[]{:S(2)}, u32[]{:S(2)}) collective-permute-start(bf16[3,3,48,256]{3,2,1,0:T(8,128)(2,1)S(1)} %get-tuple-element.55), channel_id=1, source_target_pairs={{24,16},{25,17},{26,18},{27,19},{28,20},{29,21},{30,22},{31,23}} | collective-permute-start | bytes 663560 | tf_op jit(solution)/shard_map/ppermute | solution.py:260
  78.6 17.0 %collective-permute-start.22 = (bf16[3,3,48,256]{3,2,1,0:T(8,128)(2,1)S(1)}, bf16[3,3,48,256]{3,2,1,0:T(8,128)(2,1)S(1)}, u32[]{:S(2)}, u32[]{:S(2)}) collective-permute-start(bf16[3,3,48,256]{3,2,1,0:T(8,128)(2,1)S(1)} %get-tuple-element.57), channel_id=1, source_target_pairs={{24,0},{25,1},{26,2},{27,3},{28,4},{29,5},{30,6},{31,7}} | collective-permute-start | bytes 663560 | tf_op jit(solution)/shard_map/ppermute | solution.py:260
  79.9 18.8 %collective-permute-start.23 = (bf16[3,3,48,256]{3,2,1,0:T(8,128)(2,1)S(1)}, bf16[3,3,48,256]{3,2,1,0:T(8,128)(2,1)S(1)}, u32[]{:S(2)}, u32[]{:S(2)}) collective-permute-start(bf16[3,3,48,256]{3,2,1,0:T(8,128)(2,1)S(1)} %get-tuple-element.58), channel_id=1, source_target_pairs={{24,8},{25,9},{26,10},{27,11},{28,12},{29,13},{30,14},{31,15}} | collective-permute-start | bytes 663560 | tf_op jit(solution)/shard_map/ppermute | solution.py:260
  80.6 18.1 %collective-permute-start.24 = (bf16[3,3,48,256]{3,2,1,0:T(8,128)(2,1)S(1)}, bf16[3,3,48,256]{3,2,1,0:T(8,128)(2,1)S(1)}, u32[]{:S(2)}, u32[]{:S(2)}) collective-permute-start(bf16[3,3,48,256]{3,2,1,0:T(8,128)(2,1)S(1)} %get-tuple-element.59), channel_id=1, source_target_pairs={{24,16},{25,17},{26,18},{27,19},{28,20},{29,21},{30,22},{31,23}} | collective-permute-start | bytes 663560 | tf_op jit(solution)/shard_map/ppermute | solution.py:260
  83.1 18.3 %collective-permute-start.30 = (bf16[1,3,48,256]{3,2,1,0:T(8,128)(2,1)S(1)}, bf16[1,3,48,256]{3,2,1,0:T(8,128)(2,1)S(1)}, u32[]{:S(2)}, u32[]{:S(2)}) collective-permute-start(bf16[1,3,48,256]{3,2,1,0:T(8,128)(2,1)S(1)} %get-tuple-element.51.refs_3_), channel_id=1, source_target_pairs={{24,7},{25,6},{26,5},{27,4},{28,3},{29,2},{30,1},{31,0}} | collective-permute-start | bytes 221192 | tf_op jit(solution)/shard_map/ppermute | solution.py:260
  95.6 9.5 %collective-permute-start.31 = (bf16[1,3,48,256]{3,2,1,0:T(8,128)(2,1)S(1)}, bf16[1,3,48,256]{3,2,1,0:T(8,128)(2,1)S(1)}, u32[]{:S(2)}, u32[]{:S(2)}) collective-permute-start(bf16[1,3,48,256]{3,2,1,0:T(8,128)(2,1)S(1)} %get-tuple-element.67), channel_id=1, source_target_pairs={{24,15},{25,14},{26,13},{27,12},{28,11},{29,10},{30,9},{31,8}} | collective-permute-start | bytes 221192 | tf_op jit(solution)/shard_map/ppermute | solution.py:260
  (20 other events, 110.2 us)

commit v4 on v3

--- a/solution.py
+++ b/solution.py
@@ -8,6 +8,8 @@
 
 epsilon = 1e-05
 STREAMS = 2
+ALONE = 2
+SIZES = (4, 2)
 SMALL_VMEM = 12 * 1024 * 1024
 VMEM_LIMIT = 24 * 1024 * 1024
 
@@ -90,7 +92,8 @@
     mean_square = jnp.sum(rows * rows * inverse, axis=1, keepdims=True)
     lowered = (rows * lax.rsqrt(mean_square + epsilon) * gain).astype(jnp.bfloat16)
     projected = jnp.dot(lowered, weight[0], preferred_element_type=jnp.float32)
-    gate = projected * jax.nn.sigmoid(projected)
+    half = 0.5 * projected
+    gate = half + half * jnp.tanh(half)
     done = (rows + jnp.where(inverse > 0.0, gate, 0.0)).astype(jnp.bfloat16)
     if forwards:
         outs.pop(0)[0] = done
@@ -174,10 +177,10 @@
 
 def schedule(rep_count):
     order = [0, 1, 4, 3, 5] + list(range(6, rep_count)) + [2]
-    early = order[:-2]
-    size = max(3, -(-len(early) // 4))
-    groups = [early[at : at + size] for at in range(0, len(early), size)]
-    return order, groups, order[-2:]
+    early = order[:-ALONE]
+    sizes = SIZES if sum(SIZES) == len(early) else [-(-len(early) // 4)] * 4
+    groups = [early[sum(sizes[:g]) : sum(sizes[: g + 1])] for g in range(len(sizes))]
+    return order, groups, order[-ALONE:]
 
 
 def on_device(tokens, replica_of_row, widths, placement, gains, weights):

time: 119 us -> 118 us (level)
  starting transfers between devices: 56.1 us -> 54.3 us
    ppermute x5, starting transfers between devices: 7.69 us -> 4.81 us  [traded(): return lax.ppermute(x, 'rep', [(d, d ^ i) for d in range(rep_count)])]
    ppermute x14, waiting for transfers between devices: 23.2 us -> 24.9 us  [sent_back(): piece = lax.ppermute(piece, ('section', 'rep'), hops)]
where the time goes in v4:
time: 118 us; the launch traced here: 117 us
  starting transfers between devices  54.3 us (46%)
  waiting for transfers between devices  32.4 us (27%)
  Pallas kernels  28.9 us (24%)
  local copies, waits for them, and re-layouts  1.24 us (1%)
    ppermute x12, starting transfers between devices, on_device(): inbound[n + STREAMS] = lax.ppermute(made[0], 'section', forward)  26.8 us
    ppermute x14, waiting for transfers between devices, sent_back(): piece = lax.ppermute(piece, ('section', 'rep'), hops)  24.9 us
    pallas_call x14, Pallas kernels, layer(): pl.pallas_call(functools.partial(layer_kernel, first is not None, arrived...  24.8 us
    ppermute x14, starting transfers between devices, sent_back(): piece = lax.ppermute(piece, ('section', 'rep'), hops)  12.9 us
    ppermute x7, starting transfers between devices, arriving(): return lax.ppermute(x, ('section', 'rep'), hops)  9.75 us
    ppermute x5, starting transfers between devices, traded(): return lax.ppermute(x, 'rep', [(d, d ^ i) for d in range(rep_count)])  4.81 us
    ppermute x12, waiting for transfers between devices, on_device(): inbound[n + STREAMS] = lax.ppermute(made[0], 'section', forward)  4.67 us
    ppermute x7, waiting for transfers between devices, arriving(): return lax.ppermute(x, ('section', 'rep'), hops)  2.53 us
  transfers between devices with their start and end apart: 38, of which 10 were waited for; matrix products, arithmetic and copies ran while one was open for 0% of the time, Pallas kernels for 22%

profile of v4, /device:TPU:0, one launch (start us, length us, event | category | flops | bytes accessed | tf_op | source)
XLA Modules:
  0.0 117.3 jit_solution(7489268288161448048)
XLA Ops:
  1.3 2.1 %dispatch.1 = (s32[4,1,128]{2,1,0:T(1,128)S(1)}, f32[3,2,1024]{2,1,0:T(2,128)S(1)}, bf16[3,48,1024]{2,1,0:T(8,128)(2,1)S(1)}, bf16[3,48,1024]{2,1,0:T(8,128)(2,1...) custom-call(s32[16]{0:T(128)S(1)} %copy-done.4, ...), custom_call_target="tpu_custom_call" | custom-call | flops 1207959552 | bytes 3407872 | tf_op jit(solution)/shard_map/dispatch/pallas_call | solution.py:213
  5.7 4.5 %collective-permute-start.6 = (bf16[3,48,1024]{2,1,0:T(8,128)(2,1)S(1)}, bf16[3,48,1024]{2,1,0:T(8,128)(2,1)S(1)}, u32[]{:S(2)}, u32[]{:S(2)}) collective-permute-start(bf16[3,48,1024]{2,1,0:T(8,128)(2,1)S(1)} %layer.14.refs_3_), channel_id=1, source_target_pairs={{0,8},{1,9},{2,10},{3,11},{4,12},{5,13},{6,14},{7,15}} | collective-permute-start | bytes 884744 | tf_op jit(solution)/shard_map/ppermute | solution.py:293
  17.3 2.5 %collective-permute-done.5.refs_0_ = bf16[3,48,1024]{2,1,0:T(8,128)(2,1)S(1)} collective-permute-done((bf16[3,48,1024]{2,1,0:T(8,128)(2,1)S(1)}, bf16[3,48,1024]{2,1,0:T(8,128)(2,1)S(1)}, u32[]{:S(2)}, u32[]{:S(2)}) %collective-permute-start.5) | collective-permute-done | bytes 294944 | tf_op jit(solution)/shard_map/ppermute | solution.py:248
  19.8 1.8 %layer.16.refs_4_ = bf16[3,48,1024]{2,1,0:T(8,128)(2,1)S(1)} custom-call(bf16[3,48,1024]{2,1,0:T(8,128)(2,1)S(1)} %collective-permute-done.5.refs_0_, bf16[3,48,1024]{2,1,0:T(8,128)(2,1)S(1)} %collective-permute-done.6.refs_1_, f32[3,2,1024]{2,1,0:T(2,128)S(1)} %get-tuple-element.41.refs_1_.refs_2_.refs_4_, bf16[3,1024,1024]{2,1,0:T(8,128)(2,1)S(1)} %bitcast.5, ...), custom_call_target="tpu_custom_call" | custom-call | flops 301989888 | bytes 7176192 | tf_op jit(solution)/shard_map/layer/pallas_call | solution.py:121
  21.6 1.9 %collective-permute-start.9 = (bf16[3,48,1024]{2,1,0:T(8,128)(2,1)S(1)}, bf16[3,48,1024]{2,1,0:T(8,128)(2,1)S(1)}, u32[]{:S(2)}, u32[]{:S(2)}) collective-permute-start(bf16[3,48,1024]{2,1,0:T(8,128)(2,1)S(1)} %layer.16.refs_4_), channel_id=1, source_target_pairs={{0,8},{8,16},{1,9},{9,17},{2,10},{10,18},{3,11},{11,19},{4,12},{12... | collective-permute-start | bytes 884744 | tf_op jit(solution)/shard_map/ppermute | solution.py:293
  23.5 2.8 %collective-permute-start.2 = (bf16[3,48,1024]{2,1,0:T(8,128)(2,1)S(1)}, bf16[3,48,1024]{2,1,0:T(8,128)(2,1)S(1)}, u32[]{:S(2)}, u32[]{:S(2)}) collective-permute-start(bf16[3,48,1024]{2,1,0:T(8,128)(2,1)S(1)} %get-tuple-element.44), channel_id=1, source_target_pairs={{0,6},{1,7},{2,4},{3,5},{4,2},{5,3},{6,0},{7,1},{8,9},{9,8},{10,11... | collective-permute-start | bytes 884744 | tf_op jit(solution)/shard_map/ppermute | solution.py:248
  31.0 1.8 %layer.18.refs_4_ = bf16[3,48,1024]{2,1,0:T(8,128)(2,1)S(1)} custom-call(bf16[3,48,1024]{2,1,0:T(8,128)(2,1)S(1)} %collective-permute-done.8.refs_0_, bf16[3,48,1024]{2,1,0:T(8,128)(2,1)S(1)} %collective-permute-done.9.refs_1_, f32[3,2,1024]{2,1,0:T(2,128)S(1)} %get-tuple-element.41.refs_1_.refs_2_.refs_4_, bf16[3,1024,1024]{2,1,0:T(8,128)(2,1)S(1)} %bitcast.7, ...), custom_call_target="tpu_custom_call" | custom-call | flops 301989888 | bytes 7176192 | tf_op jit(solution)/shard_map/layer/pallas_call | solution.py:121
  32.8 3.3 %collective-permute-start.12 = (bf16[3,48,1024]{2,1,0:T(8,128)(2,1)S(1)}, bf16[3,48,1024]{2,1,0:T(8,128)(2,1)S(1)}, u32[]{:S(2)}, u32[]{:S(2)}) collective-permute-start(bf16[3,48,1024]{2,1,0:T(8,128)(2,1)S(1)} %layer.18.refs_4_), channel_id=1, source_target_pairs={{0,8},{8,16},{16,24},{1,9},{9,17},{17,25},{2,10},{10,18},{18,26},{... | collective-permute-start | bytes 884744 | tf_op jit(solution)/shard_map/ppermute | solution.py:293
  36.1 1.8 %collective-permute-start.1 = (bf16[3,48,1024]{2,1,0:T(8,128)(2,1)S(1)}, bf16[3,48,1024]{2,1,0:T(8,128)(2,1)S(1)}, u32[]{:S(2)}, u32[]{:S(2)}) collective-permute-start(bf16[3,48,1024]{2,1,0:T(8,128)(2,1)S(1)} %get-tuple-element.43), channel_id=1, source_target_pairs={{0,2},{1,3},{2,0},{3,1},{4,6},{5,7},{6,4},{7,5},{8,9},{9,8},{10,11... | collective-permute-start | bytes 884744 | tf_op jit(solution)/shard_map/ppermute | solution.py:248
  37.9 1.8 %layer.19.refs_4_ = bf16[3,48,1024]{2,1,0:T(8,128)(2,1)S(1)} custom-call(bf16[3,48,1024]{2,1,0:T(8,128)(2,1)S(1)} %collective-permute-done.2.refs_0_, bf16[3,48,1024]{2,1,0:T(8,128)(2,1)S(1)} %collective-permute-done.7.refs_1_, f32[3,2,1024]{2,1,0:T(2,128)S(1)} %get-tuple-element.41.refs_1_.refs_2_.refs_4_, bf16[3,1024,1024]{2,1,0:T(8,128)(2,1)S(1)} %bitcast.8, ...), custom_call_target="tpu_custom_call" | custom-call | flops 301989888 | bytes 7176192 | tf_op jit(solution)/shard_map/layer/pallas_call | solution.py:121
  39.7 2.5 %collective-permute-start.10 = (bf16[3,48,1024]{2,1,0:T(8,128)(2,1)S(1)}, bf16[3,48,1024]{2,1,0:T(8,128)(2,1)S(1)}, u32[]{:S(2)}, u32[]{:S(2)}) collective-permute-start(bf16[3,48,1024]{2,1,0:T(8,128)(2,1)S(1)} %layer.19.refs_4_), channel_id=1, source_target_pairs={{0,8},{8,16},{16,24},{1,9},{9,17},{17,25},{2,10},{10,18},{18,26},{... | collective-permute-start | bytes 884744 | tf_op jit(solution)/shard_map/ppermute | solution.py:293
  45.2 4.4 %collective-permute-start.14 = (bf16[3,48,1024]{2,1,0:T(8,128)(2,1)S(1)}, bf16[3,48,1024]{2,1,0:T(8,128)(2,1)S(1)}, u32[]{:S(2)}, u32[]{:S(2)}) collective-permute-start(bf16[3,48,1024]{2,1,0:T(8,128)(2,1)S(1)} %layer.20.refs_4_.refs_1_), channel_id=1, source_target_pairs={{0,8},{8,16},{16,24},{1,9},{9,17},{17,25},{2,10},{10,18},{18,26},{... | collective-permute-start | bytes 884744 | tf_op jit(solution)/shard_map/ppermute | solution.py:293
  49.7 1.8 %layer.21.refs_3_.refs_2_ = bf16[3,48,1024]{2,1,0:T(8,128)(2,1)S(1)} custom-call(bf16[3,48,1024]{2,1,0:T(8,128)(2,1)S(1)} %collective-permute-done.1.refs_0_, bf16[3,48,1024]{2,1,0:T(8,128)(2,1)S(1)} %collective-permute-done.10.refs_1_, f32[3,2,1024]{2,1,0:T(2,128)S(1)} %get-tuple-element.41.refs_1_.refs_2_.refs_4_, bf16[3,1024,1024]{2,1,0:T(8,128)(2,1)S(1)} %bitcast.10, ...), custom_call_target="tpu_custom_call" | custom-call | flops 301989888 | bytes 7176192 | tf_op jit(solution)/shard_map/layer/pallas_call | solution.py:121
  51.5 4.4 %collective-permute-start.13 = (bf16[3,48,1024]{2,1,0:T(8,128)(2,1)S(1)}, bf16[3,48,1024]{2,1,0:T(8,128)(2,1)S(1)}, u32[]{:S(2)}, u32[]{:S(2)}) collective-permute-start(bf16[3,48,1024]{2,1,0:T(8,128)(2,1)S(1)} %layer.21.refs_3_.refs_2_), channel_id=1, source_target_pairs={{0,8},{8,16},{16,24},{1,9},{9,17},{17,25},{2,10},{10,18},{18,26},{... | collective-permute-start | bytes 884744 | tf_op jit(solution)/shard_map/ppermute | solution.py:293
  58.5 2.9 %collective-permute-done.13.refs_0_ = bf16[3,48,1024]{2,1,0:T(8,128)(2,1)S(1)} collective-permute-done((bf16[3,48,1024]{2,1,0:T(8,128)(2,1)S(1)}, bf16[3,48,1024]{2,1,0:T(8,128)(2,1)S(1)}, u32[]{:S(2)}, u32[]{:S(2)}) %collective-permute-start.13) | collective-permute-done | bytes 294944 | tf_op jit(solution)/shard_map/ppermute | solution.py:293
  61.4 1.8 %layer.23 = (bf16[3,48,1024]{2,1,0:T(8,128)(2,1)S(1)}, bf16[4,3,48,256]{3,2,1,0:T(8,128)(2,1)S(1)}, bf16[4,3,48,256]{3,2,1,0:T(8,128)(2,1)S(1)}, bf16[4,3,48,256...) custom-call(bf16[3,48,1024]{2,1,0:T(8,128)(2,1)S(1)} %collective-permute-done.13.refs_0_, ...), custom_call_target="tpu_custom_call" | custom-call | flops 301989888 | bytes 7176192 | tf_op jit(solution)/shard_map/layer/pallas_call | solution.py:121
  64.0 1.8 %layer.24.refs_1_.refs_4_ = bf16[3,48,1024]{2,1,0:T(8,128)(2,1)S(1)} custom-call(bf16[3,48,1024]{2,1,0:T(8,128)(2,1)S(1)} %collective-permute-done.16.refs_0_, f32[3,2,1024]{2,1,0:T(2,128)S(1)} %get-tuple-element.41.refs_1_.refs_2_.refs_4_, bf16[3,1024,1024]{2,1,0:T(8,128)(2,1)S(1)} %bitcast.13, bf16[3,48,1024]{2,1,0:T(8,128)(2,1)S(1)} %get-tuple-element.49.refs_3_), custom_call_target="tpu_custom_call" | custom-call | flops 301989888 | bytes 7176192 | tf_op jit(solution)/shard_map/layer/pallas_call | solution.py:121
  69.1 1.8 %layer.25 = (bf16[3,48,1024]{2,1,0:T(8,128)(2,1)S(1)}, bf16[2,3,48,256]{3,2,1,0:T(8,128)(2,1)S(1)}, bf16[2,3,48,256]{3,2,1,0:T(8,128)(2,1)S(1)}, bf16[2,3,48,256...) custom-call(bf16[3,48,1024]{2,1,0:T(8,128)(2,1)S(1)} %collective-permute-done.15.refs_0_, ...), custom_call_target="tpu_custom_call" | custom-call | flops 301989888 | bytes 7176192 | tf_op jit(solution)/shard_map/layer/pallas_call | solution.py:121
  72.9 8.4 %collective-permute-done.19.refs_0_ = bf16[4,3,48,256]{3,2,1,0:T(8,128)(2,1)S(1)} collective-permute-done((bf16[4,3,48,256]{3,2,1,0:T(8,128)(2,1)S(1)}, bf16[4,3,48,256]{3,2,1,0:T(8,128)(2,1)S(1)}, u32[]{:S(2)}, u32[]{:S(2)}) %collective-permute-start.19) | collective-permute-done | bytes 294944 | tf_op jit(solution)/shard_map/ppermute | solution.py:263
  82.7 1.8 %layer.26 = (bf16[1,3,48,256]{3,2,1,0:T(8,128)(2,1)S(1)}, bf16[1,3,48,256]{3,2,1,0:T(8,128)(2,1)S(1)}, bf16[1,3,48,256]{3,2,1,0:T(8,128)(2,1)S(1)}, bf16[1,3,48,256]{3,2,1,0:T(8,128)(2,1)S(1)}) custom-call(bf16[3,48,1024]{2,1,0:T(8,128)(2,1)S(1)} %collective-permute-done.18.refs_0_, f32[3,2,1024]{2,1,0:T(2,128)S(1)} %get-tuple-element.41.refs_1_.refs_2_.refs_4_, ...), custom_call_target="tpu_custom_call" | custom-call | flops 301989888 | bytes 7176192 | tf_op jit(solution)/shard_map/layer/pallas_call | solution.py:121
  85.8 11.4 %collective-permute-done.22.refs_4_ = bf16[2,3,48,256]{3,2,1,0:T(8,128)(2,1)S(1)} collective-permute-done((bf16[2,3,48,256]{3,2,1,0:T(8,128)(2,1)S(1)}, bf16[2,3,48,256]{3,2,1,0:T(8,128)(2,1)S(1)}, u32[]{:S(2)}, u32[]{:S(2)}) %collective-permute-start.22) | collective-permute-done | bytes 147488 | tf_op jit(solution)/shard_map/ppermute | solution.py:263
  98.5 1.8 %layer.27 = (bf16[1,3,48,256]{3,2,1,0:T(8,128)(2,1)S(1)}, bf16[1,3,48,256]{3,2,1,0:T(8,128)(2,1)S(1)}, bf16[1,3,48,256]{3,2,1,0:T(8,128)(2,1)S(1)}, bf16[1,3,48,256]{3,2,1,0:T(8,128)(2,1)S(1)}) custom-call(bf16[3,48,1024]{2,1,0:T(8,128)(2,1)S(1)} %collective-permute-done.17.refs_0_, f32[3,2,1024]{2,1,0:T(2,128)S(1)} %get-tuple-element.41.refs_1_.refs_2_.refs_4_, ...), custom_call_target="tpu_custom_call" | custom-call | flops 301989888 | bytes 7176192 | tf_op jit(solution)/shard_map/layer/pallas_call | solution.py:121
  101.5 2.2 %collective-permute-start.27 = (bf16[3,48,256]{2,1,0:T(8,128)(2,1)S(1)}, bf16[3,48,256]{2,1,0:T(8,128)(2,1)S(1)}, u32[]{:S(2)}, u32[]{:S(2)}) collective-permute-start(bf16[3,48,256]{2,1,0:T(8,128)(2,1)S(1)} %get-tuple-element.64), channel_id=1, source_target_pairs={{0,3},{1,2},{2,1},{3,0},{4,7},{5,6},{6,5},{7,4},{8,11},{9,10},{10,... | collective-permute-start | bytes 221192 | tf_op jit(solution)/shard_map/ppermute | solution.py:236
  111.2 5.0 %collective-permute-done.34.refs_5_ = bf16[1,3,48,256]{3,2,1,0:T(8,128)(2,1)S(1)} collective-permute-done((bf16[1,3,48,256]{3,2,1,0:T(8,128)(2,1)S(1)}, bf16[1,3,48,256]{3,2,1,0:T(8,128)(2,1)S(1)}, u32[]{:S(2)}, u32[]{:S(2)}) %collective-permute-start.34) | collective-permute-done | bytes 73760 | tf_op jit(solution)/shard_map/ppermute | solution.py:263
  (84 shorter events, 40.6 us)
Async XLA Ops:
  3.4 9.4 %collective-permute-start = (bf16[3,48,1024]{2,1,0:T(8,128)(2,1)S(1)}, bf16[3,48,1024]{2,1,0:T(8,128)(2,1)S(1)}, u32[]{:S(2)}, u32[]{:S(2)}) collective-permute-start(bf16[3,48,1024]{2,1,0:T(8,128)(2,1)S(1)} %get-tuple-element.40), channel_id=1, source_target_pairs={{0,1},{1,0},{2,3},{3,2},{4,5},{5,4},{6,7},{7,6},{8,9},{9,8},{10,11... | collective-permute-start | bytes 884744 | tf_op jit(solution)/shard_map/ppermute | solution.py:248
  5.7 11.6 %collective-permute-start.6 = (bf16[3,48,1024]{2,1,0:T(8,128)(2,1)S(1)}, bf16[3,48,1024]{2,1,0:T(8,128)(2,1)S(1)}, u32[]{:S(2)}, u32[]{:S(2)}) collective-permute-start(bf16[3,48,1024]{2,1,0:T(8,128)(2,1)S(1)} %layer.14.refs_3_), channel_id=1, source_target_pairs={{0,8},{1,9},{2,10},{3,11},{4,12},{5,13},{6,14},{7,15}} | collective-permute-start | bytes 884744 | tf_op jit(solution)/shard_map/ppermute | solution.py:293
  10.2 9.6 %collective-permute-start.5 = (bf16[3,48,1024]{2,1,0:T(8,128)(2,1)S(1)}, bf16[3,48,1024]{2,1,0:T(8,128)(2,1)S(1)}, u32[]{:S(2)}, u32[]{:S(2)}) collective-permute-start(bf16[3,48,1024]{2,1,0:T(8,128)(2,1)S(1)} %get-tuple-element.46), channel_id=1, source_target_pairs={{0,4},{1,5},{2,6},{3,7},{4,0},{5,1},{6,2},{7,3},{8,9},{9,8},{10,11... | collective-permute-start | bytes 884744 | tf_op jit(solution)/shard_map/ppermute | solution.py:248
  11.8 14.5 %collective-permute-start.3 = (bf16[3,48,1024]{2,1,0:T(8,128)(2,1)S(1)}, bf16[3,48,1024]{2,1,0:T(8,128)(2,1)S(1)}, u32[]{:S(2)}, u32[]{:S(2)}) collective-permute-start(bf16[3,48,1024]{2,1,0:T(8,128)(2,1)S(1)} %get-tuple-element.45), channel_id=1, source_target_pairs={{0,3},{1,2},{2,1},{3,0},{4,7},{5,6},{6,5},{7,4},{8,9},{9,8},{10,11... | collective-permute-start | bytes 884744 | tf_op jit(solution)/shard_map/ppermute | solution.py:248
  14.6 11.7 %collective-permute-start.4 = (bf16[3,48,1024]{2,1,0:T(8,128)(2,1)S(1)}, bf16[3,48,1024]{2,1,0:T(8,128)(2,1)S(1)}, u32[]{:S(2)}, u32[]{:S(2)}) collective-permute-start(bf16[3,48,1024]{2,1,0:T(8,128)(2,1)S(1)} %layer.15.token), channel_id=1, source_target_pairs={{0,8},{1,9},{2,10},{3,11},{4,12},{5,13},{6,14},{7,15}} | collective-permute-start | bytes 884744 | tf_op jit(solution)/shard_map/ppermute | solution.py:293
  15.9 15.1 %collective-permute-start.8 = (bf16[3,48,1024]{2,1,0:T(8,128)(2,1)S(1)}, bf16[3,48,1024]{2,1,0:T(8,128)(2,1)S(1)}, u32[]{:S(2)}, u32[]{:S(2)}) collective-permute-start(bf16[3,48,1024]{2,1,0:T(8,128)(2,1)S(1)} %get-tuple-element.47), channel_id=1, source_target_pairs={{0,5},{1,4},{2,7},{3,6},{4,1},{5,0},{6,3},{7,2},{8,9},{9,8},{10,11... | collective-permute-start | bytes 884744 | tf_op jit(solution)/shard_map/ppermute | solution.py:248
  21.6 9.4 %collective-permute-start.9 = (bf16[3,48,1024]{2,1,0:T(8,128)(2,1)S(1)}, bf16[3,48,1024]{2,1,0:T(8,128)(2,1)S(1)}, u32[]{:S(2)}, u32[]{:S(2)}) collective-permute-start(bf16[3,48,1024]{2,1,0:T(8,128)(2,1)S(1)} %layer.16.refs_4_), channel_id=1, source_target_pairs={{0,8},{8,16},{1,9},{9,17},{2,10},{10,18},{3,11},{11,19},{4,12},{12... | collective-permute-start | bytes 884744 | tf_op jit(solution)/shard_map/ppermute | solution.py:293
  23.5 14.4 %collective-permute-start.2 = (bf16[3,48,1024]{2,1,0:T(8,128)(2,1)S(1)}, bf16[3,48,1024]{2,1,0:T(8,128)(2,1)S(1)}, u32[]{:S(2)}, u32[]{:S(2)}) collective-permute-start(bf16[3,48,1024]{2,1,0:T(8,128)(2,1)S(1)} %get-tuple-element.44), channel_id=1, source_target_pairs={{0,6},{1,7},{2,4},{3,5},{4,2},{5,3},{6,0},{7,1},{8,9},{9,8},{10,11... | collective-permute-start | bytes 884744 | tf_op jit(solution)/shard_map/ppermute | solution.py:248
  28.1 9.9 %collective-permute-start.7 = (bf16[3,48,1024]{2,1,0:T(8,128)(2,1)S(1)}, bf16[3,48,1024]{2,1,0:T(8,128)(2,1)S(1)}, u32[]{:S(2)}, u32[]{:S(2)}) collective-permute-start(bf16[3,48,1024]{2,1,0:T(8,128)(2,1)S(1)} %layer.17.refs_4_), channel_id=1, source_target_pairs={{0,8},{8,16},{1,9},{9,17},{2,10},{10,18},{3,11},{11,19},{4,12},{12... | collective-permute-start | bytes 884744 | tf_op jit(solution)/shard_map/ppermute | solution.py:293
  29.8 12.4 %collective-permute-start.11 = (bf16[3,48,1024]{2,1,0:T(8,128)(2,1)S(1)}, bf16[3,48,1024]{2,1,0:T(8,128)(2,1)S(1)}, u32[]{:S(2)}, u32[]{:S(2)}) collective-permute-start(bf16[3,48,1024]{2,1,0:T(8,128)(2,1)S(1)} %get-tuple-element.48), channel_id=1, source_target_pairs={{0,7},{1,6},{2,5},{3,4},{4,3},{5,2},{6,1},{7,0},{8,9},{9,8},{10,11... | collective-permute-start | bytes 884744 | tf_op jit(solution)/shard_map/ppermute | solution.py:248
  32.8 10.6 %collective-permute-start.12 = (bf16[3,48,1024]{2,1,0:T(8,128)(2,1)S(1)}, bf16[3,48,1024]{2,1,0:T(8,128)(2,1)S(1)}, u32[]{:S(2)}, u32[]{:S(2)}) collective-permute-start(bf16[3,48,1024]{2,1,0:T(8,128)(2,1)S(1)} %layer.18.refs_4_), channel_id=1, source_target_pairs={{0,8},{8,16},{16,24},{1,9},{9,17},{17,25},{2,10},{10,18},{18,26},{... | collective-permute-start | bytes 884744 | tf_op jit(solution)/shard_map/ppermute | solution.py:293
  36.1 13.5 %collective-permute-start.1 = (bf16[3,48,1024]{2,1,0:T(8,128)(2,1)S(1)}, bf16[3,48,1024]{2,1,0:T(8,128)(2,1)S(1)}, u32[]{:S(2)}, u32[]{:S(2)}) collective-permute-start(bf16[3,48,1024]{2,1,0:T(8,128)(2,1)S(1)} %get-tuple-element.43), channel_id=1, source_target_pairs={{0,2},{1,3},{2,0},{3,1},{4,6},{5,7},{6,4},{7,5},{8,9},{9,8},{10,11... | collective-permute-start | bytes 884744 | tf_op jit(solution)/shard_map/ppermute | solution.py:248
  39.7 10.0 %collective-permute-start.10 = (bf16[3,48,1024]{2,1,0:T(8,128)(2,1)S(1)}, bf16[3,48,1024]{2,1,0:T(8,128)(2,1)S(1)}, u32[]{:S(2)}, u32[]{:S(2)}) collective-permute-start(bf16[3,48,1024]{2,1,0:T(8,128)(2,1)S(1)} %layer.19.refs_4_), channel_id=1, source_target_pairs={{0,8},{8,16},{16,24},{1,9},{9,17},{17,25},{2,10},{10,18},{18,26},{... | collective-permute-start | bytes 884744 | tf_op jit(solution)/shard_map/ppermute | solution.py:293
  45.2 10.8 %collective-permute-start.14 = (bf16[3,48,1024]{2,1,0:T(8,128)(2,1)S(1)}, bf16[3,48,1024]{2,1,0:T(8,128)(2,1)S(1)}, u32[]{:S(2)}, u32[]{:S(2)}) collective-permute-start(bf16[3,48,1024]{2,1,0:T(8,128)(2,1)S(1)} %layer.20.refs_4_.refs_1_), channel_id=1, source_target_pairs={{0,8},{8,16},{16,24},{1,9},{9,17},{17,25},{2,10},{10,18},{18,26},{... | collective-permute-start | bytes 884744 | tf_op jit(solution)/shard_map/ppermute | solution.py:293
  51.5 9.9 %collective-permute-start.13 = (bf16[3,48,1024]{2,1,0:T(8,128)(2,1)S(1)}, bf16[3,48,1024]{2,1,0:T(8,128)(2,1)S(1)}, u32[]{:S(2)}, u32[]{:S(2)}) collective-permute-start(bf16[3,48,1024]{2,1,0:T(8,128)(2,1)S(1)} %layer.21.refs_3_.refs_2_), channel_id=1, source_target_pairs={{0,8},{8,16},{16,24},{1,9},{9,17},{17,25},{2,10},{10,18},{18,26},{... | collective-permute-start | bytes 884744 | tf_op jit(solution)/shard_map/ppermute | solution.py:293
  66.4 15.0 %collective-permute-start.19 = (bf16[4,3,48,256]{3,2,1,0:T(8,128)(2,1)S(1)}, bf16[4,3,48,256]{3,2,1,0:T(8,128)(2,1)S(1)}, u32[]{:S(2)}, u32[]{:S(2)}) collective-permute-start(bf16[4,3,48,256]{3,2,1,0:T(8,128)(2,1)S(1)} %get-tuple-element.53), channel_id=1, source_target_pairs={{24,0},{25,1},{26,2},{27,3},{28,4},{29,5},{30,6},{31,7}} | collective-permute-start | bytes 884744 | tf_op jit(solution)/shard_map/ppermute | solution.py:263
  67.7 14.3 %collective-permute-start.20 = (bf16[4,3,48,256]{3,2,1,0:T(8,128)(2,1)S(1)}, bf16[4,3,48,256]{3,2,1,0:T(8,128)(2,1)S(1)}, u32[]{:S(2)}, u32[]{:S(2)}) collective-permute-start(bf16[4,3,48,256]{3,2,1,0:T(8,128)(2,1)S(1)} %get-tuple-element.54), channel_id=1, source_target_pairs={{24,8},{25,9},{26,10},{27,11},{28,12},{29,13},{30,14},{31,15}} | collective-permute-start | bytes 884744 | tf_op jit(solution)/shard_map/ppermute | solution.py:263
  68.4 16.1 %collective-permute-start.21 = (bf16[4,3,48,256]{3,2,1,0:T(8,128)(2,1)S(1)}, bf16[4,3,48,256]{3,2,1,0:T(8,128)(2,1)S(1)}, u32[]{:S(2)}, u32[]{:S(2)}) collective-permute-start(bf16[4,3,48,256]{3,2,1,0:T(8,128)(2,1)S(1)} %get-tuple-element.55), channel_id=1, source_target_pairs={{24,16},{25,17},{26,18},{27,19},{28,20},{29,21},{30,22},{31,23}} | collective-permute-start | bytes 884744 | tf_op jit(solution)/shard_map/ppermute | solution.py:263
  70.9 26.9 %collective-permute-start.17 = (bf16[3,48,1024]{2,1,0:T(8,128)(2,1)S(1)}, bf16[3,48,1024]{2,1,0:T(8,128)(2,1)S(1)}, u32[]{:S(2)}, u32[]{:S(2)}) collective-permute-start(bf16[3,48,1024]{2,1,0:T(8,128)(2,1)S(1)} %get-tuple-element.50.refs_3_), channel_id=1, source_target_pairs={{16,24},{17,25},{18,26},{19,27},{20,28},{21,29},{22,30},{23,31}} | collective-permute-start | bytes 884744 | tf_op jit(solution)/shard_map/ppermute | solution.py:293
  71.6 25.5 %collective-permute-start.22 = (bf16[2,3,48,256]{3,2,1,0:T(8,128)(2,1)S(1)}, bf16[2,3,48,256]{3,2,1,0:T(8,128)(2,1)S(1)}, u32[]{:S(2)}, u32[]{:S(2)}) collective-permute-start(bf16[2,3,48,256]{3,2,1,0:T(8,128)(2,1)S(1)} %get-tuple-element.57), channel_id=1, source_target_pairs={{24,0},{25,1},{26,2},{27,3},{28,4},{29,5},{30,6},{31,7}} | collective-permute-start | bytes 442376 | tf_op jit(solution)/shard_map/ppermute | solution.py:263
  81.4 18.9 %collective-permute-start.23 = (bf16[2,3,48,256]{3,2,1,0:T(8,128)(2,1)S(1)}, bf16[2,3,48,256]{3,2,1,0:T(8,128)(2,1)S(1)}, u32[]{:S(2)}, u32[]{:S(2)}) collective-permute-start(bf16[2,3,48,256]{3,2,1,0:T(8,128)(2,1)S(1)} %get-tuple-element.58), channel_id=1, source_target_pairs={{24,8},{25,9},{26,10},{27,11},{28,12},{29,13},{30,14},{31,15}} | collective-permute-start | bytes 442376 | tf_op jit(solution)/shard_map/ppermute | solution.py:263
  82.0 18.3 %collective-permute-start.24 = (bf16[2,3,48,256]{3,2,1,0:T(8,128)(2,1)S(1)}, bf16[2,3,48,256]{3,2,1,0:T(8,128)(2,1)S(1)}, u32[]{:S(2)}, u32[]{:S(2)}) collective-permute-start(bf16[2,3,48,256]{3,2,1,0:T(8,128)(2,1)S(1)} %get-tuple-element.59), channel_id=1, source_target_pairs={{24,16},{25,17},{26,18},{27,19},{28,20},{29,21},{30,22},{31,23}} | collective-permute-start | bytes 442376 | tf_op jit(solution)/shard_map/ppermute | solution.py:263
  84.5 17.0 %collective-permute-start.30 = (bf16[1,3,48,256]{3,2,1,0:T(8,128)(2,1)S(1)}, bf16[1,3,48,256]{3,2,1,0:T(8,128)(2,1)S(1)}, u32[]{:S(2)}, u32[]{:S(2)}) collective-permute-start(bf16[1,3,48,256]{3,2,1,0:T(8,128)(2,1)S(1)} %get-tuple-element.51.refs_3_), channel_id=1, source_target_pairs={{24,7},{25,6},{26,5},{27,4},{28,3},{29,2},{30,1},{31,0}} | collective-permute-start | bytes 221192 | tf_op jit(solution)/shard_map/ppermute | solution.py:263
  106.9 9.4 %collective-permute-start.34 = (bf16[1,3,48,256]{3,2,1,0:T(8,128)(2,1)S(1)}, bf16[1,3,48,256]{3,2,1,0:T(8,128)(2,1)S(1)}, u32[]{:S(2)}, u32[]{:S(2)}) collective-permute-start(bf16[1,3,48,256]{3,2,1,0:T(8,128)(2,1)S(1)} %get-tuple-element.52.token), channel_id=1, source_target_pairs={{24,2},{25,3},{26,0},{27,1},{28,6},{29,7},{30,4},{31,5}} | collective-permute-start | bytes 221192 | tf_op jit(solution)/shard_map/ppermute | solution.py:263
  (20 other events, 96.3 us)
